TPU v7x, 32 devices: a whole 2x2x4 slice. The times are simulated.
32 devices in a mesh: ka: 4 (over x, core), rows: 8 (over z, y).
Axes of the slice: x: 2, y: 2, z: 4, core: 2. Of those that a mesh axis runs over, the one named last changes fastest.
Arguments:
- hoppings: bfloat16 [8, 384, 128, 128], P('rows', 'ka'), may hold values from -0.09375 to 0.09375
- tile_rows: int32 [8, 384], P('rows', 'ka'), may hold values from 0 to 95, as said below
- tile_cols: int32 [8, 384], P('rows', 'ka'), may hold values from 0 to 95, as said below
- tile_lats: int32 [8, 384], P('rows', 'ka'), may hold values from 0 to 8
- tile_counts: int32 [8, 4], P('rows', 'ka'), may hold values from 48 to 96, as said below
- phase_angle: float32 [8, 9], P('ka'), may hold values from -3.140625 to 3.140625
- vectors: bfloat16 [8, 2, 12288, 256], P('ka', None, 'rows'), may hold values from -6 to 6
Outputs:
- bloch_product: float32 [8, 2, 12288, 256], P('ka', None, 'rows')
Inputs may be any that keep to these rules, and one draw needn't show every extreme that they name: `tile_rows`: slots of row block r (first index) hold tile rows r * 12 to (r + 1) * 12 - 1; several slots may name the same block. `tile_cols`: the cyclic distance between a slot's tile column and its tile row is at most 16, and both distances 16 occur in every row block. `tile_counts`: the live slots of a device are the first ones of its part of the list; some device has all 96 live.
All inputs are finite; a program needn't handle non-finite values.
Results may differ from a plain program's by a relative error of at most 0.0029.
Values may be sent and summed in bfloat16 or wider, within the bound.
A program may use at most 320 MiB of HBM per device.

v0:
```python
import functools

import jax
import jax.numpy as jnp
from jax import lax
from jax.experimental import pallas as pl
from jax.experimental.pallas import tpu as pltpu
from jax.sharding import PartitionSpec as P

NLAT = 9
BAND = 16
GROUP = 4
DEPTH = 4
MESH = pl.DeviceIdType.MESH


def spans(total, size):
    return [(start, min(size, total - start)) for start in range(0, total, size)]


def exchange_kernel(group_size, row_shards, hop, meta, vec, all_hop, all_meta, win,
                    hop_own, meta_own, send_sem, recv_sem, local_sem):
    slots = hop.shape[0]
    row_tiles = vec.shape[2]
    ka = lax.axis_index("ka")
    row = lax.axis_index("rows")
    odd = lax.rem(row, 2)
    even = 1 - odd
    sign = 1 - 2 * odd
    partner = ka + 1 - 2 * lax.rem(ka, 2)
    reach = (BAND + row_tiles - 1) // row_tiles
    depth_of = lambda d: min(row_tiles, BAND - (d - 1) * row_tiles)

    def at_row(step):
        return {"ka": ka, "rows": lax.rem(row + step + 2 * row_shards, row_shards)}

    def at_ka(other):
        return {"ka": other, "rows": row}

    across = [lax.rem(ka + 2 * h, group_size) for h in range(1, group_size // 2)]
    others = [lax.rem(ka + h, group_size) for h in range(1, group_size)]
    forwarding = row_tiles <= BAND and row_shards % 2 == 0 and reach >= 2
    peers = [at_ka(o) for o in others]
    if forwarding:
        peers.append(at_row(sign))
    else:
        peers += [at_row(1), at_row(-1)]
    for d in range(2, reach + 1):
        peers += [at_row(d), at_row(-d)]

    barrier = pltpu.get_barrier_semaphore()
    for peer in peers:
        pl.semaphore_signal(barrier, inc=1, device_id=peer, device_id_type=MESH)

    fetch_hop = pltpu.make_async_copy(hop, hop_own, local_sem.at[0])
    fetch_meta = pltpu.make_async_copy(meta, meta_own, local_sem.at[1])
    fetch_hop.start()
    fetch_meta.start()
    pl.semaphore_wait(barrier, len(peers))

    made = []

    def send(src, dst, device):
        n = len(made)
        copy = pltpu.make_async_remote_copy(
            src_ref=src, dst_ref=dst, send_sem=send_sem.at[n], recv_sem=recv_sem.at[n],
            device_id=device, device_id_type=MESH)
        copy.start()
        made.append(copy)
        return copy

    received = set()

    def arrived(copy):
        copy.wait_recv()
        received.add(id(copy))

    def vec_send(tile, count, step):
        send_to = -step * row_tiles + tile + BAND
        return send(vec.at[:, :, pl.ds(tile, count)], win.at[:, :, pl.ds(send_to, count)], at_row(step))

    def vec_pass(source, tile, count, step):
        here = source * row_tiles + tile + BAND
        there = (source - step) * row_tiles + tile + BAND
        return send(win.at[:, :, pl.ds(here, count)], win.at[:, :, pl.ds(there, count)], at_row(step))

    near_parts = []
    if forwarding:
        second = depth_of(2)
        extra = second // 2
        main = row_tiles - extra
        parts = spans(main, 2)
        near_parts.append(vec_send(even * extra + parts[0][0], parts[0][1], sign))
        turned = vec_send(odd * (row_tiles - extra), extra, -2 * sign) if extra else None
    hop_parts = []
    hop_spans = spans(slots, max(1, slots // 12))
    for h, other in enumerate(across):
        for start, count in hop_spans:
            hop_parts.append((ka + 2 * (h + 1), start, count, send(
                hop.at[pl.ds(start, count)], all_hop.at[ka, pl.ds(start, count)], at_ka(other))))
    for other in others:
        send(meta, all_meta.at[ka], at_ka(other))
    if forwarding:
        for start, count in parts[1:]:
            near_parts.append(vec_send(even * extra + start, count, sign))
        if extra:
            vec_send(odd * (row_tiles - extra), extra, sign)
        vec_send(even * (row_tiles - second), second, 2 * sign)
        if second > extra:
            vec_send(even * extra + odd * (row_tiles - second), second - extra, -2 * sign)
    else:
        first = depth_of(1)
        vec_send(0, first, -1)
        vec_send(row_tiles - first, first, 1)
        if reach >= 2:
            vec_send(0, depth_of(2), -2)
            vec_send(row_tiles - depth_of(2), depth_of(2), 2)
    for d in range(3, reach + 1):
        vec_send(0, depth_of(d), -d)
        vec_send(row_tiles - depth_of(d), depth_of(d), d)
    for start, count in hop_spans:
        send(hop.at[pl.ds(start, count)], all_hop.at[ka, pl.ds(start, count)], at_ka(partner))

    fetch_hop.wait()
    fetch_meta.wait()
    store_hop = pltpu.make_async_copy(hop_own, all_hop.at[ka], local_sem.at[0])
    store_meta = pltpu.make_async_copy(meta_own, all_meta.at[ka], local_sem.at[1])
    store_hop.start()
    store_meta.start()

    def pass_hop(n):
        owner, start, count, copy = hop_parts[n]
        owner = lax.rem(owner, group_size)
        arrived(copy)
        block = all_hop.at[owner, pl.ds(start, count)]
        send(block, block, at_ka(partner))

    done = 0
    if forwarding:
        for n, copy in enumerate(near_parts):
            arrived(copy)
            start, count = parts[n]
            vec_pass(sign, odd * extra + start, count, 2 * sign)
            if n == 1 and extra:
                arrived(turned)
                vec_pass(2 * sign, odd * (row_tiles - extra), extra, sign)
            until = len(hop_parts) * (n + 1) // (len(near_parts) + 1)
            while done < until:
                pass_hop(done)
                done += 1
        if len(near_parts) < 2 and extra:
            arrived(turned)
            vec_pass(2 * sign, odd * (row_tiles - extra), extra, sign)
    while done < len(hop_parts):
        pass_hop(done)
        done += 1

    store_hop.wait()
    store_meta.wait()
    for copy in made:
        if id(copy) not in received:
            copy.wait_recv()
    for copy in made:
        copy.wait_send()


def exchange(group_size, row_shards, hop, meta, vec):
    slots = hop.shape[0]
    width = vec.shape[2] + 2 * BAND
    return pl.pallas_call(
        functools.partial(exchange_kernel, group_size, row_shards),
        out_shape=(
            jax.ShapeDtypeStruct((group_size,) + hop.shape, hop.dtype),
            jax.ShapeDtypeStruct((group_size,) + meta.shape, meta.dtype),
            jax.ShapeDtypeStruct(vec.shape[:2] + (width,) + vec.shape[3:], vec.dtype),
        ),
        in_specs=[pl.BlockSpec(memory_space=pl.ANY)] * 3,
        out_specs=(pl.BlockSpec(memory_space=pl.ANY),) * 3,
        scratch_shapes=[
            pltpu.VMEM(hop.shape, hop.dtype),
            pltpu.VMEM(meta.shape, meta.dtype),
            pltpu.SemaphoreType.DMA((96,)),
            pltpu.SemaphoreType.DMA((96,)),
            pltpu.SemaphoreType.DMA((2,)),
        ],
        compiler_params=pltpu.CompilerParams(
            collective_id=0, has_side_effects=True, vmem_limit_bytes=60 * 2**20),
        name="exchange",
    )(hop, meta, vec)


def product_kernel(group_count, order, places, group_rows, coef, hop, vec, win, out,
                   vwin, acc, tiles, mats, tile_sem, vec_sem, out_sem):
    kpoints = vec.shape[0]
    row_tiles = vec.shape[2]
    groups = group_count[0]
    edge = vec.shape[3]

    def tile_copies(g):
        slot = lax.rem(g, DEPTH)
        return [
            pltpu.make_async_copy(hop.at[order[g * GROUP + j]], tiles.at[slot, j], tile_sem.at[slot, j])
            for j in range(GROUP)
        ]

    regions = [
        (win.at[:, :, pl.ds(0, BAND)], vwin.at[:, :, pl.ds(0, BAND)]),
        (vec, vwin.at[:, :, pl.ds(BAND, row_tiles)]),
        (win.at[:, :, pl.ds(BAND + row_tiles, BAND)], vwin.at[:, :, pl.ds(BAND + row_tiles, BAND)]),
    ]
    loads = [pltpu.make_async_copy(s, d, vec_sem.at[n]) for n, (s, d) in enumerate(regions)]
    for copy in loads:
        copy.start()
    for ahead in range(DEPTH - 1):
        @pl.when(ahead < groups)
        def _(ahead=ahead):
            for copy in tile_copies(ahead):
                copy.start()

    def clear(i, _):
        for k in range(kpoints):
            for part in range(2):
                acc[k, part, i] = jnp.zeros(acc.shape[3:], acc.dtype)
        return 0

    lax.fori_loop(0, row_tiles, clear, 0)
    for copy in loads:
        copy.wait()

    def step(g, _):
        @pl.when(g + DEPTH - 1 < groups)
        def _():
            for copy in tile_copies(g + DEPTH - 1):
                copy.start()

        for copy in tile_copies(g):
            copy.wait()
        slot = lax.rem(g, DEPTH)
        target = group_rows[g]
        for k in range(kpoints):
            for j in range(GROUP):
                n = g * GROUP + j
                tile = tiles[slot, j].astype(jnp.float32)
                cosine = (coef[2 * k, n] * tile).astype(jnp.bfloat16)
                sine = coef[2 * k + 1, n] * tile
                left = j * 2 * edge
                mats[k, :edge, left:left + edge] = cosine
                mats[k, edge:, left + edge:left + 2 * edge] = cosine
                mats[k, edge:, left:left + edge] = sine.astype(jnp.bfloat16)
                mats[k, :edge, left + edge:left + 2 * edge] = (-sine).astype(jnp.bfloat16)
        for k in range(kpoints):
            stacked = jnp.concatenate(
                [vwin[k, part, places[g * GROUP + j]] for j in range(GROUP) for part in range(2)],
                axis=0)
            result = jnp.dot(mats[k], stacked, preferred_element_type=jnp.float32)
            for part in range(2):
                acc[k, part, target] += result[part * edge:(part + 1) * edge]
        return 0

    lax.fori_loop(0, groups, step, 0)
    store = pltpu.make_async_copy(acc, out, out_sem)
    store.start()
    store.wait()


def product(group_count, order, places, group_rows, coef, hop, vec, win):
    kpoints, _, row_tiles, edge, vec_count = vec.shape
    smem = pl.BlockSpec(memory_space=pltpu.SMEM)
    return pl.pallas_call(
        product_kernel,
        out_shape=jax.ShapeDtypeStruct(vec.shape, jnp.float32),
        in_specs=[smem] * 5 + [pl.BlockSpec(memory_space=pl.ANY)] * 3,
        out_specs=pl.BlockSpec(memory_space=pl.ANY),
        scratch_shapes=[
            pltpu.VMEM(win.shape, win.dtype),
            pltpu.VMEM(vec.shape, jnp.float32),
            pltpu.VMEM((DEPTH, GROUP, edge, edge), hop.dtype),
            pltpu.VMEM((kpoints, 2 * edge, 2 * GROUP * edge), jnp.bfloat16),
            pltpu.SemaphoreType.DMA((DEPTH, GROUP)),
            pltpu.SemaphoreType.DMA((3,)),
            pltpu.SemaphoreType.DMA,
        ],
        compiler_params=pltpu.CompilerParams(vmem_limit_bytes=60 * 2**20),
        name="product",
    )(group_count, order, places, group_rows, coef, hop, vec, win)


def body(hoppings, tile_rows, tile_cols, tile_lats, tile_counts, phase_angle, vectors):
    edge = hoppings.shape[2]
    per_device = hoppings.shape[1]
    group_size = lax.axis_size("ka")
    row_shards = lax.axis_size("rows")
    kpoints, _, orbitals, vec_count = vectors.shape
    row_tiles = orbitals // edge
    total_tiles = row_tiles * row_shards
    row_start = lax.axis_index("rows") * row_tiles
    slots = group_size * per_device

    lanes = -(-per_device // 128) * 128
    live = lax.broadcasted_iota(jnp.int32, (1, per_device), 1) < tile_counts
    rows = jnp.where(live, tile_rows - row_start, row_tiles)
    place = jnp.mod(tile_cols - row_start + BAND, total_tiles)
    meta = jnp.concatenate([rows, place, tile_lats, jnp.zeros((5, per_device), jnp.int32)], axis=0)
    meta = jnp.pad(meta, ((0, 0), (0, lanes - per_device)))
    vec = vectors.reshape(kpoints, 2, row_tiles, edge, vec_count)
    all_hop, all_meta, win = exchange(group_size, row_shards, hoppings[0], meta, vec)

    all_hop = all_hop.reshape(slots, edge, edge)
    slot_rows = all_meta[:, 0, :per_device].reshape(slots)
    slot_place = all_meta[:, 1, :per_device].reshape(slots)
    slot_lats = all_meta[:, 2, :per_device].reshape(slots)
    group_max = slots // GROUP + row_tiles
    in_row = slot_rows[None, :] == lax.iota(jnp.int32, row_tiles)[:, None]
    row_counts = jnp.sum(in_row.astype(jnp.int32), axis=1)
    row_groups = jnp.maximum((row_counts + GROUP - 1) // GROUP, 1)
    ends = jnp.sum(
        jnp.where(lax.iota(jnp.int32, row_tiles)[None, :] <= lax.iota(jnp.int32, row_tiles)[:, None],
                  row_groups[None, :], 0), axis=1)
    starts = ends - row_groups
    before = lax.iota(jnp.int32, slots)[None, :] < lax.iota(jnp.int32, slots)[:, None]
    same = slot_rows[None, :] == slot_rows[:, None]
    rank = jnp.sum((before & same).astype(jnp.int32), axis=1)
    base = jnp.sum(jnp.where(in_row, starts[:, None], 0), axis=0)
    position = jnp.where(slot_rows < row_tiles, base * GROUP + rank, -1)
    hit = lax.iota(jnp.int32, group_max * GROUP)[:, None] == position[None, :]

    def arranged(values):
        return jnp.sum(jnp.where(hit, values[None, :], 0), axis=1)

    order = arranged(lax.iota(jnp.int32, slots))
    places = arranged(slot_place)
    lats = arranged(slot_lats + 1) - 1
    group_rows = jnp.minimum(
        jnp.sum((lax.iota(jnp.int32, group_max)[:, None] >= ends[None, :]).astype(jnp.int32), axis=1),
        row_tiles - 1)
    weights = jnp.stack([jnp.cos(phase_angle), jnp.sin(phase_angle)], axis=1).reshape(2 * kpoints, -1)
    coef = jnp.sum(
        jnp.where(lats[None, :, None] == lax.iota(jnp.int32, weights.shape[1]), weights[:, None, :], 0.0),
        axis=2)
    out = product(ends[-1:], order, places, group_rows, coef, all_hop, vec, win)
    return out.reshape(kpoints, 2, orbitals, vec_count)


def solution(mesh):
    return jax.shard_map(
        body,
        mesh=mesh,
        in_specs=(
            P("rows", "ka", None, None),
            P("rows", "ka"),
            P("rows", "ka"),
            P("rows", "ka"),
            P("rows", "ka"),
            P("ka", None),
            P("ka", None, "rows", None),
        ),
        out_specs=P("ka", None, "rows", None),
        check_vma=False,
    )
```

profile of v0, /device:TPU:0, one launch (start us, length us, event | category | flops | bytes accessed | tf_op | source)
XLA Modules:
  0.0 175.3 jit_solution(12872762361348207156)
XLA Ops:
  0.7 0.7 and_select_fusion.1
  1.3 0.1 pad.10.clone
  1.4 0.7 cosine_bitcast_fusion
  2.2 0.7 add_add_fusion
  2.9 0.6 pad.4.meta
  3.5 0.1 copy.10
  3.6 110.8 %exchange.1 = (bf16[4,96,128,128]{3,2,1,0:T(8,128)(2,1)}, s32[4,8,128]{2,1,0:T(8,128)}, bf16[2,2,44,128,256]{4,3,2,1,0:T(8,128)(2,1)}) custom-call(bf16[96,128,128]{2,1,0:T(8,128)(2,1)} %bitcast.14, s32[8,128]{1,0:T(8,128)} %pad.4.meta, bf16[2,2,12,128,256]{4,3,2,1,0:T(8,128)(2,1)} %bitcast.12), custom_call_target="tpu_custom_call" | custom-call | tf_op jit(solution)/shard_map/exchange/pallas_call | solution.py:170
  114.4 0.9 add_reduce_fusion
  115.3 0.1 add.70
  115.4 0.1 eq.61
  115.5 0.1 convert_reduce_fusion.1
  115.6 0.1 select_reduce_fusion.5
  115.7 0.6 slice.13.group_count
  116.4 0.1 convert_reduce_fusion.2
  116.4 0.5 broadcast_minimum_fusion.group_rows
  117.0 0.1 select_reduce_fusion.4
  117.1 0.2 convert_reduce_fusion
  117.3 0.1 broadcast_in_dim.107
  117.4 0.9 select_reduce_fusion
  118.3 0.7 select_reduce_fusion.3.coef
  119.0 56.3 %product.1 = f32[2,2,12,128,256]{4,3,2,1,0:T(8,128)} custom-call(s32[1]{0:T(128)} %slice.13.group_count, s32[432]{0:T(512)} %get-tuple-element.16.order, s32[432]{0:T(512)} %get-tuple-element.15.places, s32[108]{0:T(128)} %broadcast_minimum_fusion.group_rows, f32[4,432]{1,0:T(4,128)} %select_reduce_fusion.3.coef, bf16[384,128,128]{2,1,0:T(8,128)(2,1)} %bitcast.11, ...), custom_call_target="tpu_custom_call" | custom-call | tf_op jit(solution)/shard_map/product/pallas_call | solution.py:269
  (8 shorter events, 0.1 us)
where the time goes:
time: 173 us; the launch traced here: 175 us
  Pallas kernels  167 us (97%)
  other arithmetic  5.13 us (3%)
  local copies, waits for them, and re-layouts  2.36 us (1%)
    pallas_call x1, Pallas kernels, exchange(): pl.pallas_call(functools.partial(exchange_kernel, group_size, row_shards)...  111 us
    pallas_call x1, Pallas kernels, product(): pl.pallas_call(product_kernel, out_shape=jax.ShapeDtypeStruct(vec.shape,...  56.3 us

commit v1 on v0

--- a/solution.py
+++ b/solution.py
@@ -87,7 +87,7 @@
     near_parts = []
     if forwarding:
         second = depth_of(2)
-        extra = second // 2
+        extra = min(second, row_tiles - 2)
         main = row_tiles - extra
         parts = spans(main, 2)
         near_parts.append(vec_send(even * extra + parts[0][0], parts[0][1], sign))

time: 173 us -> 161 us (0.931)
  Pallas kernels: 167 us -> 155 us
    pallas_call x1, Pallas kernels: 111 us -> 99.6 us  [exchange(): pl.pallas_call(functools.partial(exchange_kernel, group_size, row_shards)...]
where the time goes in v1:
time: 161 us; the launch traced here: 163 us
  Pallas kernels  155 us (96%)
  other arithmetic  5.13 us (3%)
  local copies, waits for them, and re-layouts  2.36 us (1%)
    pallas_call x1, Pallas kernels, exchange(): pl.pallas_call(functools.partial(exchange_kernel, group_size, row_shards)...  99.6 us
    pallas_call x1, Pallas kernels, product(): pl.pallas_call(product_kernel, out_shape=jax.ShapeDtypeStruct(vec.shape,...  55.7 us

profile of v1, /device:TPU:0, one launch (start us, length us, event | category | flops | bytes accessed | tf_op | source)
XLA Modules:
  0.0 163.5 jit_solution(3869989996455483425)
XLA Ops:
  0.7 0.7 and_select_fusion.1
  1.3 0.1 pad.10.clone
  1.4 0.7 cosine_bitcast_fusion
  2.2 0.7 add_add_fusion
  2.9 0.6 pad.4.meta
  3.5 0.1 copy.10
  3.6 99.6 %exchange.1 = (bf16[4,96,128,128]{3,2,1,0:T(8,128)(2,1)}, s32[4,8,128]{2,1,0:T(8,128)}, bf16[2,2,44,128,256]{4,3,2,1,0:T(8,128)(2,1)}) custom-call(bf16[96,128,128]{2,1,0:T(8,128)(2,1)} %bitcast.14, s32[8,128]{1,0:T(8,128)} %pad.4.meta, bf16[2,2,12,128,256]{4,3,2,1,0:T(8,128)(2,1)} %bitcast.12), custom_call_target="tpu_custom_call" | custom-call | tf_op jit(solution)/shard_map/exchange/pallas_call | solution.py:170
  103.2 0.9 add_reduce_fusion
  104.0 0.1 add.70
  104.1 0.1 eq.61
  104.2 0.1 convert_reduce_fusion.1
  104.3 0.1 select_reduce_fusion.5
  104.4 0.6 slice.13.group_count
  105.1 0.1 convert_reduce_fusion.2
  105.2 0.5 broadcast_minimum_fusion.group_rows
  105.7 0.1 select_reduce_fusion.4
  105.8 0.2 convert_reduce_fusion
  106.0 0.1 broadcast_in_dim.107
  106.1 0.9 select_reduce_fusion
  107.1 0.7 select_reduce_fusion.3.coef
  107.7 55.7 %product.1 = f32[2,2,12,128,256]{4,3,2,1,0:T(8,128)} custom-call(s32[1]{0:T(128)} %slice.13.group_count, s32[432]{0:T(512)} %get-tuple-element.16.order, s32[432]{0:T(512)} %get-tuple-element.15.places, s32[108]{0:T(128)} %broadcast_minimum_fusion.group_rows, f32[4,432]{1,0:T(4,128)} %select_reduce_fusion.3.coef, bf16[384,128,128]{2,1,0:T(8,128)(2,1)} %bitcast.11, ...), custom_call_target="tpu_custom_call" | custom-call | tf_op jit(solution)/shard_map/product/pallas_call | solution.py:269
  (8 shorter events, 0.1 us)

commit v2 on v1

v2 whole, which is shorter than its diff:
```python
import functools

import jax
import jax.numpy as jnp
from jax import lax
from jax.experimental import pallas as pl
from jax.experimental.pallas import tpu as pltpu
from jax.sharding import PartitionSpec as P

NLAT = 9
BAND = 16
GROUP = 4
STAGES = 2
MESH = pl.DeviceIdType.MESH


def spans(total, size):
    return [(start, min(size, total - start)) for start in range(0, total, size)]


def exchange_kernel(group_size, row_shards, hop, meta, vec, all_hop, all_meta, win,
                    send_sem, recv_sem, local_sem):
    slots = hop.shape[0]
    row_tiles = vec.shape[2]
    ka = lax.axis_index("ka")
    row = lax.axis_index("rows")
    odd = lax.rem(row, 2)
    even = 1 - odd
    sign = 1 - 2 * odd
    partner = ka + 1 - 2 * lax.rem(ka, 2)
    reach = (BAND + row_tiles - 1) // row_tiles
    depth_of = lambda d: min(row_tiles, BAND - (d - 1) * row_tiles)

    def at_row(step):
        return {"ka": ka, "rows": lax.rem(row + step + 2 * row_shards, row_shards)}

    def at_ka(other):
        return {"ka": other, "rows": row}

    across = [lax.rem(ka + 2 * h, group_size) for h in range(1, group_size // 2)]
    others = [lax.rem(ka + h, group_size) for h in range(1, group_size)]
    forwarding = row_tiles <= BAND and row_shards % 2 == 0 and reach >= 2
    peers = [at_ka(o) for o in others]
    if forwarding:
        peers.append(at_row(sign))
    else:
        peers += [at_row(1), at_row(-1)]
    for d in range(2, reach + 1):
        peers += [at_row(d), at_row(-d)]

    barrier = pltpu.get_barrier_semaphore()
    for peer in peers:
        pl.semaphore_signal(barrier, inc=1, device_id=peer, device_id_type=MESH)

    local = [
        pltpu.make_async_copy(hop, all_hop.at[pl.ds(ka * slots, slots)], local_sem.at[0]),
        pltpu.make_async_copy(meta, all_meta.at[ka], local_sem.at[1]),
        pltpu.make_async_copy(vec, win.at[:, :, pl.ds(BAND, row_tiles)], local_sem.at[2]),
    ]
    for copy in local:
        copy.start()
    pl.semaphore_wait(barrier, len(peers))

    made = []

    def send(src, dst, device):
        n = len(made)
        copy = pltpu.make_async_remote_copy(
            src_ref=src, dst_ref=dst, send_sem=send_sem.at[n], recv_sem=recv_sem.at[n],
            device_id=device, device_id_type=MESH)
        copy.start()
        made.append(copy)
        return copy

    received = set()

    def arrived(copy):
        copy.wait_recv()
        received.add(id(copy))

    def vec_send(tile, count, step):
        send_to = -step * row_tiles + tile + BAND
        return send(vec.at[:, :, pl.ds(tile, count)], win.at[:, :, pl.ds(send_to, count)], at_row(step))

    def vec_pass(source, tile, count, step):
        here = source * row_tiles + tile + BAND
        there = (source - step) * row_tiles + tile + BAND
        return send(win.at[:, :, pl.ds(here, count)], win.at[:, :, pl.ds(there, count)], at_row(step))

    near_parts = []
    if forwarding:
        second = depth_of(2)
        extra = min(second, row_tiles - 2)
        main = row_tiles - extra
        parts = spans(main, 2)
        near_parts.append(vec_send(even * extra + parts[0][0], parts[0][1], sign))
        turned = vec_send(odd * (row_tiles - extra), extra, -2 * sign) if extra else None
    hop_parts = []
    hop_spans = spans(slots, max(1, slots // 12))
    for h, other in enumerate(across):
        for start, count in hop_spans:
            hop_parts.append((ka + 2 * (h + 1), start, count, send(
                hop.at[pl.ds(start, count)], all_hop.at[pl.ds(ka * slots + start, count)], at_ka(other))))
    for other in others:
        send(meta, all_meta.at[ka], at_ka(other))
    if forwarding:
        for start, count in parts[1:]:
            near_parts.append(vec_send(even * extra + start, count, sign))
        if extra:
            vec_send(odd * (row_tiles - extra), extra, sign)
        vec_send(even * (row_tiles - second), second, 2 * sign)
        if second > extra:
            vec_send(even * extra + odd * (row_tiles - second), second - extra, -2 * sign)
    else:
        first = depth_of(1)
        vec_send(0, first, -1)
        vec_send(row_tiles - first, first, 1)
        if reach >= 2:
            vec_send(0, depth_of(2), -2)
            vec_send(row_tiles - depth_of(2), depth_of(2), 2)
    for d in range(3, reach + 1):
        vec_send(0, depth_of(d), -d)
        vec_send(row_tiles - depth_of(d), depth_of(d), d)
    for start, count in hop_spans:
        send(hop.at[pl.ds(start, count)], all_hop.at[pl.ds(ka * slots + start, count)], at_ka(partner))

    def pass_hop(n):
        owner, start, count, copy = hop_parts[n]
        owner = lax.rem(owner, group_size)
        arrived(copy)
        block = all_hop.at[pl.ds(owner * slots + start, count)]
        send(block, block, at_ka(partner))

    done = 0
    if forwarding:
        for n, copy in enumerate(near_parts):
            arrived(copy)
            start, count = parts[n]
            vec_pass(sign, odd * extra + start, count, 2 * sign)
            if n == 1 and extra:
                arrived(turned)
                vec_pass(2 * sign, odd * (row_tiles - extra), extra, sign)
            until = len(hop_parts) * (n + 1) // (len(near_parts) + 1)
            while done < until:
                pass_hop(done)
                done += 1
        if len(near_parts) < 2 and extra:
            arrived(turned)
            vec_pass(2 * sign, odd * (row_tiles - extra), extra, sign)
    while done < len(hop_parts):
        pass_hop(done)
        done += 1

    for copy in local:
        copy.wait()
    for copy in made:
        if id(copy) not in received:
            copy.wait_recv()
    for copy in made:
        copy.wait_send()


def exchange(group_size, row_shards, hop, meta, vec):
    slots = hop.shape[0]
    width = vec.shape[2] + 2 * BAND
    return pl.pallas_call(
        functools.partial(exchange_kernel, group_size, row_shards),
        out_shape=(
            pltpu.VMEM((group_size * slots,) + hop.shape[1:], hop.dtype),
            jax.ShapeDtypeStruct((group_size,) + meta.shape, meta.dtype),
            pltpu.VMEM(vec.shape[:2] + (width,) + vec.shape[3:], vec.dtype),
        ),
        in_specs=[pl.BlockSpec(memory_space=pl.ANY)] * 3,
        out_specs=(pl.BlockSpec(memory_space=pltpu.VMEM), pl.BlockSpec(memory_space=pl.ANY),
                   pl.BlockSpec(memory_space=pltpu.VMEM)),
        scratch_shapes=[
            pltpu.SemaphoreType.DMA((96,)),
            pltpu.SemaphoreType.DMA((96,)),
            pltpu.SemaphoreType.DMA((3,)),
        ],
        compiler_params=pltpu.CompilerParams(
            collective_id=0, has_side_effects=True, vmem_limit_bytes=2**20),
        name="exchange",
    )(pltpu.with_memory_space_constraint(hop, pltpu.HBM), meta,
      pltpu.with_memory_space_constraint(vec, pltpu.HBM))


def bits_of(count):
    return max(1, (count - 1).bit_length())


def arrange(meta, bucket, counts, group_size, per_device):
    slots = group_size * per_device
    buckets = counts.shape[0]
    for row in range(buckets):
        counts[row] = 0

    def take(i, _):
        for owner in range(group_size):
            row = meta[owner, 0, i]
            held = counts[row]
            bucket[row * (slots + GROUP) + held] = meta[owner, 1, i]
            counts[row] = held + 1
        return 0

    lax.fori_loop(0, per_device, take, 0, unroll=8 if per_device % 8 == 0 else 1)


def multiply(rows, group_stride, place_bits, tile_bits, pad, bucket, counts, weights, tiles, vwin, accs):
    kpoints = vwin.shape[0]

    def each_row(row, finish):
        held = counts[row]
        base = row * group_stride
        for j in range(GROUP - 1):
            bucket[base + held + j] = pad

        def step(g, _):
            for j in range(GROUP):
                code = bucket[base + g * GROUP + j]
                index = code & (2**tile_bits - 1)
                place = (code >> tile_bits) & (2**place_bits - 1)
                lattice = code >> (tile_bits + place_bits)
                tile = tiles[index].astype(jnp.float32)
                for k in range(kpoints):
                    stacked = jnp.concatenate([vwin[k, 0, place], vwin[k, 1, place]], axis=0)
                    pltpu.matmul_push_rhs(stacked, staging_register=j % 2, mxu_index=k % 2)
                    cosine = (weights[2 * k, lattice] * tile).astype(jnp.bfloat16)
                    sine = (weights[2 * k + 1, lattice] * tile).astype(jnp.bfloat16)
                    matrix = jnp.concatenate(
                        [jnp.concatenate([cosine, -sine], axis=1),
                         jnp.concatenate([sine, cosine], axis=1)], axis=0)
                    pltpu.matmul_acc_lhs(accs[k], matrix, load_staged_rhs=j % 2)
            return 0

        lax.fori_loop(0, (held + GROUP - 1) // GROUP, step, 0)
        finish(row)

    return each_row


def product_kernel(group_size, per_device, tile_bits, place_bits, pad, meta, weights, tiles, vwin, out,
                   bucket, counts, stage, out_sem):
    kpoints, _, _, edge, _ = vwin.shape
    row_tiles = out.shape[2]
    arrange(meta, bucket, counts, group_size, per_device)

    def run(*accs):
        def store(row):
            slot = lax.rem(row, STAGES)
            return pltpu.make_async_copy(stage.at[slot], out.at[:, :, row], out_sem.at[slot])

        def finish(row):
            @pl.when(row >= STAGES)
            def _():
                store(row - STAGES).wait()

            slot = lax.rem(row, STAGES)
            for k in range(kpoints):
                result = pltpu.matmul_pop(accs[k])
                for part in range(2):
                    stage[slot, k, part] = result[part * edge:(part + 1) * edge]
            store(row).start()

        each_row = multiply(row_tiles, group_size * per_device + GROUP, place_bits, tile_bits, pad, bucket, counts,
                            weights, tiles, vwin, accs)

        def one(row, _):
            each_row(row, finish)
            return 0

        lax.fori_loop(0, row_tiles, one, 0)
        for row in range(max(0, row_tiles - STAGES), row_tiles):
            store(row).wait()

    pl.run_scoped(run, *[pltpu.ACC(k % 2)((2 * edge, vwin.shape[4]), jnp.float32) for k in range(kpoints)])


def product(per_device, tile_bits, place_bits, pad, meta, weights, hop, win, row_tiles):
    kpoints, _, _, edge, vec_count = win.shape
    group_size = hop.shape[0] // per_device
    smem = pl.BlockSpec(memory_space=pltpu.SMEM)
    vmem = pl.BlockSpec(memory_space=pltpu.VMEM)
    return pl.pallas_call(
        functools.partial(product_kernel, group_size, per_device, tile_bits, place_bits, pad),
        out_shape=jax.ShapeDtypeStruct((kpoints, 2, row_tiles, edge, vec_count), jnp.float32),
        in_specs=[smem] * 2 + [vmem] * 2,
        out_specs=pl.BlockSpec(memory_space=pl.ANY),
        scratch_shapes=[
            pltpu.SMEM(((row_tiles + 1) * (hop.shape[0] + GROUP),), jnp.int32),
            pltpu.SMEM((row_tiles + 1,), jnp.int32),
            pltpu.VMEM((STAGES, kpoints, 2, edge, vec_count), jnp.float32),
            pltpu.SemaphoreType.DMA((STAGES,)),
        ],
        compiler_params=pltpu.CompilerParams(vmem_limit_bytes=12 * 2**20),
        name="product",
    )(meta, weights,
      pltpu.with_memory_space_constraint(hop, pltpu.VMEM),
      pltpu.with_memory_space_constraint(win, pltpu.VMEM))


def body(hoppings, tile_rows, tile_cols, tile_lats, tile_counts, phase_angle, vectors):
    edge = hoppings.shape[2]
    per_device = hoppings.shape[1]
    group_size = lax.axis_size("ka")
    row_shards = lax.axis_size("rows")
    kpoints, _, orbitals, vec_count = vectors.shape
    lattices = phase_angle.shape[1]
    row_tiles = orbitals // edge
    total_tiles = row_tiles * row_shards
    row_start = lax.axis_index("rows") * row_tiles
    slots = group_size * per_device
    tile_bits = bits_of(slots)
    place_bits = bits_of(row_tiles + 2 * BAND)

    lanes = -(-per_device // 128) * 128
    slot = lax.broadcasted_iota(jnp.int32, (1, per_device), 1)
    rows = jnp.where(slot < tile_counts, tile_rows - row_start, row_tiles)
    place = jnp.mod(tile_cols - row_start + BAND, total_tiles)
    code = (((tile_lats << place_bits) + place) << tile_bits) + lax.axis_index("ka") * per_device + slot
    meta = jnp.concatenate([rows, code, jnp.zeros((6, per_device), jnp.int32)], axis=0)
    meta = jnp.pad(meta, ((0, 0), (0, lanes - per_device)))
    vec = vectors.reshape(kpoints, 2, row_tiles, edge, vec_count)
    weights = jnp.stack([jnp.cos(phase_angle), jnp.sin(phase_angle)], axis=1).reshape(2 * kpoints, lattices)
    weights = jnp.pad(weights, ((0, 0), (0, 1)))
    all_hop, all_meta, win = exchange(group_size, row_shards, hoppings[0], meta, vec)
    pad = lattices << (place_bits + tile_bits)
    out = product(per_device, tile_bits, place_bits, pad, all_meta, weights, all_hop, win, row_tiles)
    return out.reshape(kpoints, 2, orbitals, vec_count)


def solution(mesh):
    return jax.shard_map(
        body,
        mesh=mesh,
        in_specs=(
            P("rows", "ka", None, None),
            P("rows", "ka"),
            P("rows", "ka"),
            P("rows", "ka"),
            P("rows", "ka"),
            P("ka", None),
            P("ka", None, "rows", None),
        ),
        out_specs=P("ka", None, "rows", None),
        check_vma=False,
    )
```

time: 161 us -> 134 us (0.83); the launches traced: 163 us -> 132 us
  Pallas kernels: 155 us -> 130 us
  other arithmetic: 5.13 us -> 0.79 us
    pallas_call x1, Pallas kernels: 55.7 us -> 30.6 us  [product(): pl.pallas_call(functools.partial(product_kernel, group_size, per_device,...]
    reduce_sum x7 -> x0, other arithmetic: 2.26 us -> none  [the longest x1 0.94 us: arranged(): return jnp.sum(jnp.where(hit, values[None, :], 0), axis=1)]
where the time goes in v2:
time: 134 us; the launch traced here: 132 us
  Pallas kernels  130 us (97%)
    pallas_call x1, Pallas kernels, exchange(): pl.pallas_call(functools.partial(exchange_kernel, group_size, row_shards)...  99.5 us
    pallas_call x1, Pallas kernels, product(): pl.pallas_call(functools.partial(product_kernel, group_size, per_device,...  30.6 us

profile of v2, /device:TPU:0, one launch (start us, length us, event | category | flops | bytes accessed | tf_op | source)
XLA Modules:
  0.0 132.4 jit_solution(4103567365092327028)
XLA Ops:
  0.7 0.7 compare_select_fusion
  1.4 0.1 pad.14.clone
  1.4 0.7 cosine_bitcast_fusion
  2.2 0.1 add_add_fusion
  2.3 99.5 %exchange.1 = (bf16[384,128,128]{2,1,0:T(8,128)(2,1)S(1)}, s32[4,8,128]{2,1,0:T(8,128)S(1)}, bf16[2,2,44,128,256]{4,3,2,1,0:T(8,128)(2,1)S(1)}) custom-call(bf16[96,128,128]{2,1,0:T(8,128)(2,1)} %bitcast.10, s32[8,128]{1,0:T(8,128)S(1)} %pad.8.meta, bf16[2,2,12,128,256]{4,3,2,1,0:T(8,128)(2,1)} %bitcast.11), custom_call_target="tpu_custom_call" | custom-call | tf_op jit(solution)/shard_map/exchange/pallas_call | solution.py:166
  101.8 30.6 %product.1 = f32[2,2,12,128,256]{4,3,2,1,0:T(8,128)} custom-call(s32[4,8,128]{2,1,0:T(8,128)S(1)} %get-tuple-element.8.meta, f32[4,10]{1,0:T(4,128)S(1)} %pad.9.weights, bf16[384,128,128]{2,1,0:T(8,128)(2,1)S(1)} %get-tuple-element.9.tiles, bf16[2,2,44,128,256]{4,3,2,1,0:T(8,128)(2,1)S(1)} %get-tuple-element.10.vwin), custom_call_target="tpu_custom_call" | custom-call | tf_op jit(solution)/shard_map/product/pallas_call | solution.py:284
  (5 shorter events, 0.0 us)

commit v3 on v2

v3 whole, which is shorter than its diff:
```python
import functools

import jax
import jax.numpy as jnp
from jax import lax
from jax.experimental import pallas as pl
from jax.experimental.pallas import tpu as pltpu
from jax.sharding import PartitionSpec as P

NLAT = 9
BAND = 16
GROUP = 4
LATE_GROUP = 2
MESH = pl.DeviceIdType.MESH


def spans(total, size):
    return [(start, min(size, total - start)) for start in range(0, total, size)]


def late_tiles(row_tiles, row_shards):
    reach = (BAND + row_tiles - 1) // row_tiles
    if row_tiles > BAND or row_shards % 2 or reach < 2:
        return 0, 0
    extra = min(row_tiles, BAND - row_tiles, row_tiles - 2)
    return min(extra, row_tiles - extra), extra


def exchange_kernel(group_size, row_shards, hop, meta, vec, all_hop, all_meta, win, *rest):
    across_tiles, beside_tiles = late_tiles(vec.shape[2], row_shards)
    if across_tiles and beside_tiles:
        across_out, beside_out, send_sem, recv_sem, local_sem = rest
    else:
        send_sem, recv_sem, local_sem = rest

    slots = hop.shape[0]
    row_tiles = vec.shape[2]
    ka = lax.axis_index("ka")
    row = lax.axis_index("rows")
    odd = lax.rem(row, 2)
    even = 1 - odd
    sign = 1 - 2 * odd
    partner = ka + 1 - 2 * lax.rem(ka, 2)
    reach = (BAND + row_tiles - 1) // row_tiles
    depth_of = lambda d: min(row_tiles, BAND - (d - 1) * row_tiles)

    def at_row(step):
        return {"ka": ka, "rows": lax.rem(row + step + 2 * row_shards, row_shards)}

    def at_ka(other):
        return {"ka": other, "rows": row}

    across = [lax.rem(ka + 2 * h, group_size) for h in range(1, group_size // 2)]
    others = [lax.rem(ka + h, group_size) for h in range(1, group_size)]
    forwarding = row_tiles <= BAND and row_shards % 2 == 0 and reach >= 2
    peers = [at_ka(o) for o in others]
    if forwarding:
        peers.append(at_row(sign))
    else:
        peers += [at_row(1), at_row(-1)]
    for d in range(2, reach + 1):
        peers += [at_row(d), at_row(-d)]

    barrier = pltpu.get_barrier_semaphore()
    for peer in peers:
        pl.semaphore_signal(barrier, inc=1, device_id=peer, device_id_type=MESH)

    local = [
        pltpu.make_async_copy(hop, all_hop.at[pl.ds(ka * slots, slots)], local_sem.at[0]),
        pltpu.make_async_copy(meta, all_meta.at[ka], local_sem.at[1]),
        pltpu.make_async_copy(vec, win.at[:, :, pl.ds(BAND, row_tiles)], local_sem.at[2]),
    ]
    for copy in local:
        copy.start()
    pl.semaphore_wait(barrier, len(peers))

    made = []

    def send(src, dst, device):
        n = len(made)
        copy = pltpu.make_async_remote_copy(
            src_ref=src, dst_ref=dst, send_sem=send_sem.at[n], recv_sem=recv_sem.at[n],
            device_id=device, device_id_type=MESH)
        copy.start()
        made.append(copy)
        return copy

    received = set()

    def arrived(copy):
        copy.wait_recv()
        received.add(id(copy))

    def vec_send(tile, count, step):
        send_to = -step * row_tiles + tile + BAND
        return send(vec.at[:, :, pl.ds(tile, count)], win.at[:, :, pl.ds(send_to, count)], at_row(step))

    def vec_pass(source, tile, count, step):
        here = source * row_tiles + tile + BAND
        there = (source - step) * row_tiles + tile + BAND
        return send(win.at[:, :, pl.ds(here, count)], win.at[:, :, pl.ds(there, count)], at_row(step))

    near_parts = []
    if forwarding:
        second = depth_of(2)
        extra = min(second, row_tiles - 2)
        main = row_tiles - extra
        kept = main - across_tiles
        parts = spans(kept, 2) + [(kept + start, count) for start, count in spans(across_tiles, 2)]

        def part_tile(parity_even, parity_odd, start, count):
            return parity_even * (extra + start) + parity_odd * (main - start - count)

        near_parts.append(vec_send(part_tile(even, odd, *parts[0]), parts[0][1], sign))
        turned = vec_send(odd * (row_tiles - extra), extra, -2 * sign) if extra else None
    hop_parts = []
    hop_spans = spans(slots, max(1, slots // 12))
    for h, other in enumerate(across):
        for start, count in hop_spans:
            hop_parts.append((ka + 2 * (h + 1), start, count, send(
                hop.at[pl.ds(start, count)], all_hop.at[pl.ds(ka * slots + start, count)], at_ka(other))))
    for other in others:
        send(meta, all_meta.at[ka], at_ka(other))
    if forwarding:
        for start, count in parts[1:]:
            near_parts.append(vec_send(part_tile(even, odd, start, count), count, sign))
        if extra and not beside_tiles:
            vec_send(odd * (row_tiles - extra), extra, sign)
        vec_send(even * (row_tiles - second), second, 2 * sign)
        if second > extra:
            vec_send(even * extra + odd * (row_tiles - second), second - extra, -2 * sign)
    else:
        first = depth_of(1)
        vec_send(0, first, -1)
        vec_send(row_tiles - first, first, 1)
        if reach >= 2:
            vec_send(0, depth_of(2), -2)
            vec_send(row_tiles - depth_of(2), depth_of(2), 2)
    for d in range(3, reach + 1):
        vec_send(0, depth_of(d), -d)
        vec_send(row_tiles - depth_of(d), depth_of(d), d)
    for start, count in hop_spans:
        send(hop.at[pl.ds(start, count)], all_hop.at[pl.ds(ka * slots + start, count)], at_ka(partner))

    def pass_hop(n):
        owner, start, count, copy = hop_parts[n]
        owner = lax.rem(owner, group_size)
        arrived(copy)
        block = all_hop.at[pl.ds(owner * slots + start, count)]
        send(block, block, at_ka(partner))

    if beside_tiles:
        local[2].wait()
        hold = pltpu.make_async_copy(
            win.at[:, :, pl.ds(BAND + odd * (row_tiles - beside_tiles), beside_tiles)], beside_out, local_sem.at[3])
        hold.start()
        local[2] = hold

    done = 0
    if forwarding:
        for n, copy in enumerate(near_parts):
            arrived(copy)
            start, count = parts[n]
            tile = part_tile(odd, even, start, count)
            if start < kept:
                vec_pass(sign, tile, count, 2 * sign)
            else:
                first = part_tile(odd, even, kept, across_tiles)
                hold = pltpu.make_async_copy(
                    win.at[:, :, pl.ds(sign * row_tiles + tile + BAND, count)],
                    across_out.at[:, :, pl.ds(tile - first, count)], local_sem.at[4 + n])
                hold.start()
                local.append(hold)
            if n == 1 and extra:
                arrived(turned)
                vec_pass(2 * sign, odd * (row_tiles - extra), extra, sign)
            until = len(hop_parts) * (n + 1) // (len(near_parts) + 1)
            while done < until:
                pass_hop(done)
                done += 1
        if len(near_parts) < 2 and extra:
            arrived(turned)
            vec_pass(2 * sign, odd * (row_tiles - extra), extra, sign)
    while done < len(hop_parts):
        pass_hop(done)
        done += 1

    for copy in local:
        copy.wait()
    for copy in made:
        if id(copy) not in received:
            copy.wait_recv()
    for copy in made:
        copy.wait_send()


def exchange(group_size, row_shards, hop, meta, vec):
    slots = hop.shape[0]
    width = vec.shape[2] + 2 * BAND
    late = tuple(
        jax.ShapeDtypeStruct(vec.shape[:2] + (count,) + vec.shape[3:], vec.dtype)
        for count in late_tiles(vec.shape[2], row_shards) if count)
    return pl.pallas_call(
        functools.partial(exchange_kernel, group_size, row_shards),
        out_shape=(
            pltpu.VMEM((group_size * slots,) + hop.shape[1:], hop.dtype),
            jax.ShapeDtypeStruct((group_size,) + meta.shape, meta.dtype),
            pltpu.VMEM(vec.shape[:2] + (width,) + vec.shape[3:], vec.dtype),
        ) + late,
        in_specs=[pl.BlockSpec(memory_space=pl.ANY)] * 3,
        out_specs=(pl.BlockSpec(memory_space=pltpu.VMEM), pl.BlockSpec(memory_space=pl.ANY),
                   pl.BlockSpec(memory_space=pltpu.VMEM)) + (pl.BlockSpec(memory_space=pl.ANY),) * len(late),
        scratch_shapes=[
            pltpu.SemaphoreType.DMA((96,)),
            pltpu.SemaphoreType.DMA((96,)),
            pltpu.SemaphoreType.DMA((16,)),
        ],
        compiler_params=pltpu.CompilerParams(
            collective_id=0, has_side_effects=True, vmem_limit_bytes=2**20),
        name="exchange",
    )(pltpu.with_memory_space_constraint(hop, pltpu.HBM), meta,
      pltpu.with_memory_space_constraint(vec, pltpu.HBM))


def bits_of(count):
    return max(1, (count - 1).bit_length())


def arrange(meta, bucket, counts, group_size, per_device):
    stride = group_size * per_device + GROUP
    for row in range(counts.shape[0]):
        counts[row] = 0

    def take(i, _):
        for owner in range(group_size):
            row = meta[owner, 0, i]
            held = counts[row]
            bucket[row * stride + held] = meta[owner, 1, i]
            counts[row] = held + 1
        return 0

    lax.fori_loop(0, per_device, take, 0, unroll=8 if per_device % 8 == 0 else 1)


def matrix_of(weights, tile, lattice, k):
    cosine = (weights[2 * k, lattice] * tile).astype(jnp.bfloat16)
    sine = (weights[2 * k + 1, lattice] * tile).astype(jnp.bfloat16)
    return jnp.concatenate(
        [jnp.concatenate([cosine, -sine], axis=1), jnp.concatenate([sine, cosine], axis=1)], axis=0)


def unpacked(bits, code):
    tile_bits, place_bits = bits
    return (code & (2**tile_bits - 1), (code >> tile_bits) & (2**place_bits - 1),
            code >> (tile_bits + place_bits))


def push(bits, code, windows, kpoints, register):
    _, place, _ = unpacked(bits, code)
    for k in range(kpoints):
        if len(windows) == 1:
            parts = [windows[0][k, part, place] for part in range(2)]
        else:
            split = windows[0].shape[2]
            near, far = jnp.minimum(place, split - 1), jnp.maximum(place - split, 0)
            parts = [jnp.where(place < split, windows[0][k, part, near], windows[1][k, part, far])
                     for part in range(2)]
        pltpu.matmul_push_rhs(jnp.concatenate(parts, axis=0), staging_register=register, mxu_index=k % 2)


def group(bits, size, at, following, bucket, weights, tiles, windows, accs):
    codes = [bucket[at + j] for j in range(size)]
    for j, code in enumerate(codes):
        push(bits, codes[j + 1] if j + 1 < size else bucket[following], windows, len(accs), (j + 1) % 2)
        index, _, lattice = unpacked(bits, code)
        tile = tiles[index].astype(jnp.float32)
        for k, acc in enumerate(accs):
            pltpu.matmul_acc_lhs(acc, matrix_of(weights, tile, lattice, k), load_staged_rhs=j % 2)


def every_row(bits, size, row_tiles, first, stride, bucket, counts, weights, tiles, windows, accs, spare, finish, done=None):
    kpoints = windows[0].shape[0]
    sets = (accs[:kpoints], accs[kpoints:])

    def one(row, now, before):
        base = (first + row) * stride
        groups = jnp.maximum((counts[first + row] + size - 1) // size, 1)
        after = jnp.minimum(row + 1, row_tiles - 1)

        def follow(g):
            return jnp.where(g + 1 < groups, base + (g + 1) * size, (first + after) * stride)

        group(bits, size, base, follow(0), bucket, weights, tiles, windows, now)
        finish(jnp.maximum(row - 1, 0), [pltpu.matmul_pop(acc) for acc in before])
        if done is not None:
            @pl.when(row > 0)
            def _():
                done(row - 1)

        def step(g, _):
            group(bits, size, base + g * size, follow(g), bucket, weights, tiles, windows, now)
            return 0

        lax.fori_loop(1, groups, step, 0)

    def pair(i, _):
        one(2 * i, sets[0], sets[1])
        one(2 * i + 1, sets[1], sets[0])
        return 0

    push(bits, bucket[first * stride], windows, kpoints, 0)
    lax.fori_loop(0, row_tiles // 2, pair, 0)
    if row_tiles % 2:
        one(row_tiles - 1, sets[0], sets[1])
    finish(row_tiles - 1, [pltpu.matmul_pop(acc) for acc in sets[1 - row_tiles % 2]])
    if done is not None:
        done(row_tiles - 1)
    nothing = jnp.zeros((spare[0].shape[0], 256), jnp.bfloat16)
    for acc in spare:
        pltpu.matmul_acc_lhs(acc, nothing, load_staged_rhs=0)
        pltpu.matmul_pop(acc)


def accumulators(kpoints, edge, vec_count):
    return ([pltpu.ACC(k % 2)((2 * edge, vec_count), jnp.float32) for k in range(kpoints)] * 2
            + [pltpu.ACC(k % 2)((16, vec_count), jnp.float32) for k in range(kpoints)])


def first_kernel(group_size, per_device, row_tiles, bits, pad, meta, weights, tiles, window, total, bucket, counts):
    kpoints, _, _, edge, vec_count = window.shape
    stride = group_size * per_device + GROUP
    arrange(meta, bucket, counts, group_size, per_device)
    for row in range(2 * row_tiles):
        for j in range(GROUP):
            bucket[row * stride + counts[row] + j] = pad

    def run(*accs):
        def finish(row, results):
            for k, result in enumerate(results):
                for part in range(2):
                    total[k, part, row] = result[part * edge:(part + 1) * edge]

        every_row(bits, GROUP, row_tiles, 0, stride, bucket, counts, weights, tiles, [window], accs[:-kpoints],
                  accs[-kpoints:], finish)

    pl.run_scoped(run, *accumulators(kpoints, edge, vec_count))


def second_kernel(stride, bits, bucket, counts, weights, tiles, total, across, beside, out, stage, out_sem):
    kpoints, _, row_tiles, edge, vec_count = total.shape

    def store(row):
        return pltpu.make_async_copy(stage.at[:, :, row], out.at[:, :, row], out_sem.at[row])

    def run(*accs):
        def finish(row, results):
            for k, result in enumerate(results):
                for part in range(2):
                    stage[k, part, row] = total[k, part, row] + result[part * edge:(part + 1) * edge]

        every_row(bits, LATE_GROUP, row_tiles, row_tiles, stride, bucket, counts, weights, tiles, [across, beside],
                  accs[:-kpoints], accs[-kpoints:], finish, lambda row: store(row).start())

    pl.run_scoped(run, *accumulators(kpoints, edge, vec_count))
    for row in range(row_tiles):
        store(row).wait()


def in_vmem(x):
    return pltpu.with_memory_space_constraint(x, pltpu.VMEM)


SMEM = pl.BlockSpec(memory_space=pltpu.SMEM)
VMEM = pl.BlockSpec(memory_space=pltpu.VMEM)
ANY = pl.BlockSpec(memory_space=pl.ANY)


def first_product(per_device, row_tiles, bits, pad, meta, weights, hop, win):
    kpoints, _, _, edge, vec_count = win.shape
    slots = hop.shape[0]
    buckets = 2 * row_tiles + 1
    work = slots * kpoints * 8 * edge * edge * vec_count
    return pl.pallas_call(
        functools.partial(first_kernel, slots // per_device, per_device, row_tiles, bits, pad),
        out_shape=(
            pltpu.VMEM((kpoints, 2, row_tiles, edge, vec_count), jnp.float32),
            jax.ShapeDtypeStruct((buckets * (slots + GROUP),), jnp.int32),
            jax.ShapeDtypeStruct((buckets,), jnp.int32),
        ),
        in_specs=[SMEM] * 2 + [VMEM] * 2,
        out_specs=(VMEM, SMEM, SMEM),
        compiler_params=pltpu.CompilerParams(vmem_limit_bytes=2**20),
        cost_estimate=pl.CostEstimate(flops=work, bytes_accessed=2**24, transcendentals=0),
        name="first",
    )(meta, weights, in_vmem(hop), in_vmem(win))


def second_product(bits, bucket, counts, weights, hop, total, across, beside):
    kpoints, _, row_tiles, edge, vec_count = total.shape
    return pl.pallas_call(
        functools.partial(second_kernel, hop.shape[0] + GROUP, bits),
        out_shape=jax.ShapeDtypeStruct(total.shape, jnp.float32),
        in_specs=[SMEM] * 3 + [VMEM] * 4,
        out_specs=ANY,
        scratch_shapes=[
            pltpu.VMEM(total.shape, jnp.float32),
            pltpu.SemaphoreType.DMA((row_tiles,)),
        ],
        compiler_params=pltpu.CompilerParams(vmem_limit_bytes=12 * 2**20),
        name="second",
    )(bucket, counts, weights, in_vmem(hop), in_vmem(total), in_vmem(across), in_vmem(beside))


def body(hoppings, tile_rows, tile_cols, tile_lats, tile_counts, phase_angle, vectors):
    edge = hoppings.shape[2]
    per_device = hoppings.shape[1]
    group_size = lax.axis_size("ka")
    row_shards = lax.axis_size("rows")
    kpoints, _, orbitals, vec_count = vectors.shape
    lattices = phase_angle.shape[1]
    row_tiles = orbitals // edge
    total_tiles = row_tiles * row_shards
    shard = lax.axis_index("rows")
    row_start = shard * row_tiles
    across_tiles, beside_tiles = late_tiles(row_tiles, row_shards)
    bits = (bits_of(group_size * per_device), bits_of(row_tiles + 2 * BAND))

    lanes = -(-per_device // 128) * 128
    slot = lax.broadcasted_iota(jnp.int32, (1, per_device), 1)
    place = jnp.mod(tile_cols - row_start + BAND, total_tiles)
    low, high = BAND - row_tiles, BAND + 2 * row_tiles
    even = lax.rem(shard, 2) == 0
    across_at = place - jnp.where(even, low, high - across_tiles)
    beside_at = place - jnp.where(even, high - beside_tiles, low)
    from_across = (across_at >= 0) & (across_at < across_tiles)
    from_beside = (beside_at >= 0) & (beside_at < beside_tiles)
    rows = tile_rows - row_start + jnp.where(from_across | from_beside, row_tiles, 0)
    rows = jnp.where(slot < tile_counts, rows, 2 * row_tiles)
    place = jnp.where(from_across, across_at, jnp.where(from_beside, across_tiles + beside_at, place))
    code = (((tile_lats << bits[1]) + place) << bits[0]) + lax.axis_index("ka") * per_device + slot
    meta = jnp.concatenate([rows, code, jnp.zeros((6, per_device), jnp.int32)], axis=0)
    meta = jnp.pad(meta, ((0, 0), (0, lanes - per_device)))
    vec = vectors.reshape(kpoints, 2, row_tiles, edge, vec_count)
    weights = jnp.stack([jnp.cos(phase_angle), jnp.sin(phase_angle)], axis=1).reshape(2 * kpoints, lattices)
    weights = jnp.pad(weights, ((0, 0), (0, 1)))
    pad = lattices << (bits[0] + bits[1])

    all_hop, all_meta, win, *late = exchange(group_size, row_shards, hoppings[0], meta, vec)
    if late:
        sign = [1 - 2 * (r % 2) for r in range(row_shards)]
        across = lax.ppermute(late[0], "rows", [(r, (r + 2 * sign[r]) % row_shards) for r in range(row_shards)])
        beside = lax.ppermute(late[1], "rows", [(r, r + sign[r]) for r in range(row_shards)])
    total, bucket, counts = first_product(per_device, row_tiles, bits, pad, all_meta, weights, all_hop, win)
    if late:
        total = second_product(bits, bucket, counts, weights, all_hop, total, across, beside)
    return total.reshape(kpoints, 2, orbitals, vec_count)


def solution(mesh):
    return jax.shard_map(
        body,
        mesh=mesh,
        in_specs=(
            P("rows", "ka", None, None),
            P("rows", "ka"),
            P("rows", "ka"),
            P("rows", "ka"),
            P("rows", "ka"),
            P("ka", None),
            P("ka", None, "rows", None),
        ),
        out_specs=P("ka", None, "rows", None),
        check_vma=False,
    )
```

time: 134 us -> 115 us (0.86); the launches traced: 132 us -> 116 us
  Pallas kernels: 130 us -> 112 us
  starting transfers between devices: 0 us -> 2.74 us
    pallas_call x1, Pallas kernels: 99.5 us -> 77.7 us  [exchange(): pl.pallas_call(functools.partial(exchange_kernel, group_size, row_shards)...]
    pallas_call x1 -> x2, Pallas kernels: 30.6 us -> 34.1 us  [the longest x1 27.1 us: first_product(): pl.pallas_call(functools.partial(first_kernel, slots // per_device, per_d...]
    ppermute x0 -> x2, starting transfers between devices: none -> 2.74 us  [the longest x1 2.68 us: body(): lax.ppermute(late[1], 'rows', [(r, r + sign[r]) for r in range(row_shards)])]
  transfers between devices with their start and end apart: 0 -> 2, of which waited for: 0 -> 0; matrix products, arithmetic and copies ran while one was open for 0% -> 0% of each run, Pallas kernels for 0% -> 23%
where the time goes in v3:
time: 115 us; the launch traced here: 116 us
  Pallas kernels  112 us (97%)
  starting transfers between devices  2.74 us (2%)
    pallas_call x1, Pallas kernels, exchange(): pl.pallas_call(functools.partial(exchange_kernel, group_size, row_shards)...  77.7 us
    pallas_call x1, Pallas kernels, first_product(): pl.pallas_call(functools.partial(first_kernel, slots // per_device, per_d...  27.1 us
    pallas_call x1, Pallas kernels, second_product(): pl.pallas_call(functools.partial(second_kernel, hop.shape[0] + GROUP, bit...  6.99 us
    ppermute x1, starting transfers between devices, body(): lax.ppermute(late[1], 'rows', [(r, r + sign[r]) for r in range(row_shards)])  2.68 us
  transfers between devices with their start and end apart: 2, of which 0 were waited for; matrix products, arithmetic and copies ran while one was open for 0% of the time, Pallas kernels for 23%

profile of v3, /device:TPU:0, one launch (start us, length us, event | category | flops | bytes accessed | tf_op | source)
XLA Modules:
  0.0 116.2 jit_solution(6349714064228065789)
XLA Ops:
  0.0 0.0 copy-start
  0.7 0.1 pad.14.clone
  0.8 0.7 compare_select_fusion
  1.5 0.1 add_add_fusion
  1.5 77.7 %exchange.1 = (bf16[384,128,128]{2,1,0:T(8,128)(2,1)S(1)}, s32[4,8,128]{2,1,0:T(8,128)S(1)}, bf16[2,2,44,128,256]{4,3,2,1,0:T(8,128)(2,1)S(1)}, bf16[2,2,4,128,2...) custom-call(bf16[96,128,128]{2,1,0:T(8,128)(2,1)} %bitcast.10, s32[8,128]{1,0:T(8,128)S(1)} %pad.8.meta, ...), custom_call_target="tpu_custom_call" | custom-call | tf_op jit(solution)/shard_map/exchange/pallas_call | solution.py:203
  79.3 0.1 collective-permute-start
  79.4 2.7 %collective-permute-start.1 = (bf16[2,2,4,128,256]{4,3,2,1,0:T(8,128)(2,1)S(1)}, bf16[2,2,4,128,256]{4,3,2,1,0:T(8,128)(2,1)S(1)}, u32[]{:S(2)}, u32[]{:S(2)}) collective-permute-start(bf16[2,2,4,128,256]{4,3,2,1,0:T(8,128)(2,1)S(1)} %get-tuple-element.20), channel_id=1, source_target_pairs={{0,1},{1,0},{2,3},{3,2},{4,5},{5,4},{6,7},{7,6},{8,9},{9,8},{10,11... | collective-permute-start | bytes 3145736 | tf_op jit(solution)/shard_map/ppermute | solution.py:452
  82.0 0.0 copy-done
  82.1 27.1 %first.1 = (f32[2,2,12,128,256]{4,3,2,1,0:T(8,128)S(1)}, s32[9700]{0:T(1024)S(1)}, s32[25]{0:T(128)S(1)}) custom-call(s32[4,8,128]{2,1,0:T(8,128)S(1)} %get-tuple-element.13.meta, f32[4,10]{1,0:T(4,128)S(1)} %pad.9.weights, bf16[384,128,128]{2,1,0:T(8,128)(2,1)S(1)} %get-tuple-element.14.tiles, bf16[2,2,44,128,256]{4,3,2,1,0:T(8,128)(2,1)S(1)} %get-tuple-element.15.window), custom_call_target="tpu_custom_call" | custom-call | flops 25769803776 | bytes 16777216 | tf_op jit(solution)/shard_map/first/pallas_call | solution.py:383
  109.2 0.0 collective-permute-done.across
  109.2 0.0 collective-permute-done.1.beside
  109.2 7.0 %second.1 = f32[2,2,12,128,256]{4,3,2,1,0:T(8,128)} custom-call(s32[9700]{0:T(1024)S(1)} %get-tuple-element.16.bucket, s32[25]{0:T(128)S(1)} %get-tuple-element.17.counts, f32[4,10]{1,0:T(4,128)S(1)} %pad.9.weights, bf16[384,128,128]{2,1,0:T(8,128)(2,1)S(1)} %get-tuple-element.14.tiles, f32[2,2,12,128,256]{4,3,2,1,0:T(8,128)S(1)} %get-tuple-element.18.total, ...), custom_call_target="tpu_custom_call" | custom-call | tf_op jit(solution)/shard_map/second/pallas_call | solution.py:400
  (6 shorter events, 0.1 us)
Async XLA Ops:
  0.0 82.0 %copy-start = (f32[2,9]{1,0:T(2,128)S(1)}, f32[2,9]{1,0:T(2,128)}, u32[]{:S(2)}) copy-start(f32[2,9]{1,0:T(2,128)} %param.12) | copy-start | bytes 220
  79.3 29.9 %collective-permute-start = (bf16[2,2,4,128,256]{4,3,2,1,0:T(8,128)(2,1)S(1)}, bf16[2,2,4,128,256]{4,3,2,1,0:T(8,128)(2,1)S(1)}, u32[]{:S(2)}, u32[]{:S(2)}) collective-permute-start(bf16[2,2,4,128,256]{4,3,2,1,0:T(8,128)(2,1)S(1)} %get-tuple-element.19), channel_id=1, source_target_pairs={{0,2},{1,7},{2,4},{3,1},{4,6},{5,3},{6,0},{7,5},{8,10},{9,15},{10,... | collective-permute-start | bytes 3145736 | tf_op jit(solution)/shard_map/ppermute | solution.py:451
  79.4 29.9 %collective-permute-start.1 = (bf16[2,2,4,128,256]{4,3,2,1,0:T(8,128)(2,1)S(1)}, bf16[2,2,4,128,256]{4,3,2,1,0:T(8,128)(2,1)S(1)}, u32[]{:S(2)}, u32[]{:S(2)}) collective-permute-start(bf16[2,2,4,128,256]{4,3,2,1,0:T(8,128)(2,1)S(1)} %get-tuple-element.20), channel_id=1, source_target_pairs={{0,1},{1,0},{2,3},{3,2},{4,5},{5,4},{6,7},{7,6},{8,9},{9,8},{10,11... | collective-permute-start | bytes 3145736 | tf_op jit(solution)/shard_map/ppermute | solution.py:452

commit v4 on v3

--- a/solution.py
+++ b/solution.py
@@ -26,15 +26,80 @@
     return min(extra, row_tiles - extra), extra
 
 
-def exchange_kernel(group_size, row_shards, hop, meta, vec, all_hop, all_meta, win, *rest):
+def column(row):
+    size = row.shape[1]
+    same = (lax.broadcasted_iota(jnp.int32, (size, size), 0) == lax.broadcasted_iota(jnp.int32, (size, size), 1))
+    return jnp.sum(jnp.where(same, jnp.broadcast_to(row, (size, size)), 0.0), axis=1, keepdims=True)
+
+
+def make_plan(row_shards, row_tiles, bits, ints, lives, plan):
+    group_size, _, _, per_device = ints.shape
+    across_tiles, beside_tiles = late_tiles(row_tiles, row_shards)
+    shard = lax.axis_index("rows")
+    row_start = shard * row_tiles
+    total_tiles = row_tiles * row_shards
+    odd = lax.rem(shard, 2)
+    even = 1 - odd
+    low, high = BAND - row_tiles, BAND + 2 * row_tiles
+    across_from = even * low + odd * (high - across_tiles)
+    beside_from = even * (high - beside_tiles) + odd * low
+    lane = lax.broadcasted_iota(jnp.int32, (1, per_device), 1)
+
+    rows, codes, row_cols, code_cols = [], [], [], []
+    for owner in range(group_size):
+        place = ints[owner, 1] - row_start + BAND
+        place = jnp.where(place < 0, place + total_tiles, place)
+        place = jnp.where(place >= total_tiles, place - total_tiles, place)
+        row = ints[owner, 0] - row_start
+        for begin, count, shift in ((across_from, across_tiles, 0), (beside_from, beside_tiles, across_tiles)):
+            if count:
+                late = (place >= begin) & (place < begin + count) & (row < row_tiles)
+                row = jnp.where(late, row + row_tiles, row)
+                place = jnp.where(late, place - begin + shift, place)
+        row = jnp.where(lane < lives[owner], row, 2 * row_tiles)
+        code = (((ints[owner, 2] + 1) << bits[1]) + place << bits[0]) + owner * per_device + lane
+        rows.append(row.astype(jnp.float32))
+        codes.append(code.astype(jnp.float32))
+        row_cols.append(column(rows[-1]))
+        code_cols.append(column(codes[-1]))
+    row_col = jnp.concatenate(row_cols, axis=0)
+    code_col = jnp.concatenate(code_cols, axis=0)
+    slots = group_size * per_device
+    buckets = -(-(2 * row_tiles + 1) // 8) * 8
+    bucket = lax.broadcasted_iota(jnp.int32, (buckets, 1), 0).astype(jnp.float32)
+    held = jnp.zeros((buckets, 1), jnp.float32)
+    for row in rows:
+        held += jnp.sum(jnp.where(bucket == row, 1.0, 0.0), axis=1, keepdims=True)
+    held = jnp.maximum(held, 1.0)
+    held = jnp.where(bucket < row_tiles, jnp.floor((held + (GROUP - 1)) * (1 / GROUP)) * GROUP,
+                     jnp.floor((held + (LATE_GROUP - 1)) * (1 / LATE_GROUP)) * LATE_GROUP)
+    index = lax.broadcasted_iota(jnp.int32, (slots, 1), 0)
+    spots = []
+    for owner, row in enumerate(rows):
+        ahead = (row_col == row) & (index < lane + owner * per_device)
+        rank = jnp.sum(jnp.where(ahead, 1.0, 0.0), axis=0, keepdims=True)
+        base = jnp.sum(jnp.where(bucket < row, held, 0.0), axis=0, keepdims=True)
+        spots.append(column(jnp.where(row < 2 * row_tiles, base + rank, -1.0)))
+    spot = jnp.concatenate(spots, axis=0)
+    wide = lax.broadcasted_iota(jnp.int32, (1, 128), 1)
+    for block in range(plan.shape[0] - 1):
+        here = spot == (wide + block * 128).astype(jnp.float32)
+        plan[block:block + 1] = jnp.sum(jnp.where(here, code_col, 0.0), axis=0, keepdims=True).astype(jnp.int32)
+    starts = jnp.sum(jnp.where(bucket < wide.astype(jnp.float32), held, 0.0), axis=0, keepdims=True)
+    plan[plan.shape[0] - 1:] = starts.astype(jnp.int32)
+
+
+def exchange_kernel(group_size, row_shards, bits, hop, tile_rows, tile_cols, tile_lats, tile_counts, vec,
+                    all_hop, plan, win, *rest):
     across_tiles, beside_tiles = late_tiles(vec.shape[2], row_shards)
     if across_tiles and beside_tiles:
-        across_out, beside_out, send_sem, recv_sem, local_sem = rest
+        across_out, beside_out, ints, lives, own_lives, send_sem, recv_sem, local_sem = rest
     else:
-        send_sem, recv_sem, local_sem = rest
+        ints, lives, own_lives, send_sem, recv_sem, local_sem = rest
 
     slots = hop.shape[0]
     row_tiles = vec.shape[2]
+    own_lives[...] = jnp.full(own_lives.shape, tile_counts[0, 0], jnp.int32)
     ka = lax.axis_index("ka")
     row = lax.axis_index("rows")
     odd = lax.rem(row, 2)
@@ -67,12 +132,15 @@
 
     local = [
         pltpu.make_async_copy(hop, all_hop.at[pl.ds(ka * slots, slots)], local_sem.at[0]),
-        pltpu.make_async_copy(meta, all_meta.at[ka], local_sem.at[1]),
+        pltpu.make_async_copy(own_lives, lives.at[ka], local_sem.at[1]),
         pltpu.make_async_copy(vec, win.at[:, :, pl.ds(BAND, row_tiles)], local_sem.at[2]),
     ]
-    for copy in local:
+    for field, source in enumerate((tile_rows, tile_cols, tile_lats)):
+        local.append(pltpu.make_async_copy(source, ints.at[ka, field], local_sem.at[4 + field]))
+    for copy in [local[0]] + local[2:]:
         copy.start()
     pl.semaphore_wait(barrier, len(peers))
+    local[1].start()
 
     made = []
 
@@ -100,6 +168,12 @@
         there = (source - step) * row_tiles + tile + BAND
         return send(win.at[:, :, pl.ds(here, count)], win.at[:, :, pl.ds(there, count)], at_row(step))
 
+    about = []
+    for other in others:
+        for field, source in enumerate((tile_rows, tile_cols, tile_lats)):
+            about.append(send(source, ints.at[ka, field], at_ka(other)))
+        about.append(send(own_lives, lives.at[ka], at_ka(other)))
+
     near_parts = []
     if forwarding:
         second = depth_of(2)
@@ -119,8 +193,6 @@
         for start, count in hop_spans:
             hop_parts.append((ka + 2 * (h + 1), start, count, send(
                 hop.at[pl.ds(start, count)], all_hop.at[pl.ds(ka * slots + start, count)], at_ka(other))))
-    for other in others:
-        send(meta, all_meta.at[ka], at_ka(other))
     if forwarding:
         for start, count in parts[1:]:
             near_parts.append(vec_send(part_tile(even, odd, start, count), count, sign))
@@ -156,6 +228,13 @@
         hold.start()
         local[2] = hold
 
+    for copy in about:
+        arrived(copy)
+    for copy in [local[1]] + local[3:]:
+        copy.wait()
+    del local[3:], local[1]
+    make_plan(row_shards, row_tiles, bits, ints, lives, plan)
+
     done = 0
     if forwarding:
         for n, copy in enumerate(near_parts):
@@ -168,7 +247,7 @@
                 first = part_tile(odd, even, kept, across_tiles)
                 hold = pltpu.make_async_copy(
                     win.at[:, :, pl.ds(sign * row_tiles + tile + BAND, count)],
-                    across_out.at[:, :, pl.ds(tile - first, count)], local_sem.at[4 + n])
+                    across_out.at[:, :, pl.ds(tile - first, count)], local_sem.at[7 + n])
                 hold.start()
                 local.append(hold)
             if n == 1 and extra:
@@ -194,52 +273,46 @@
         copy.wait_send()
 
 
-def exchange(group_size, row_shards, hop, meta, vec):
+SMEM = pl.BlockSpec(memory_space=pltpu.SMEM)
+VMEM = pl.BlockSpec(memory_space=pltpu.VMEM)
+ANY = pl.BlockSpec(memory_space=pl.ANY)
+
+
+def exchange(group_size, row_shards, bits, hop, ints, vec):
     slots = hop.shape[0]
+    per_device = ints[0].shape[1]
+    row_tiles = vec.shape[2]
+    blocks = (group_size * per_device + row_tiles * (GROUP + LATE_GROUP)) // 128 + 1
     width = vec.shape[2] + 2 * BAND
     late = tuple(
         jax.ShapeDtypeStruct(vec.shape[:2] + (count,) + vec.shape[3:], vec.dtype)
         for count in late_tiles(vec.shape[2], row_shards) if count)
     return pl.pallas_call(
-        functools.partial(exchange_kernel, group_size, row_shards),
+        functools.partial(exchange_kernel, group_size, row_shards, bits),
         out_shape=(
             pltpu.VMEM((group_size * slots,) + hop.shape[1:], hop.dtype),
-            jax.ShapeDtypeStruct((group_size,) + meta.shape, meta.dtype),
+            pltpu.VMEM((blocks + 1, 128), jnp.int32),
             pltpu.VMEM(vec.shape[:2] + (width,) + vec.shape[3:], vec.dtype),
         ) + late,
-        in_specs=[pl.BlockSpec(memory_space=pl.ANY)] * 3,
-        out_specs=(pl.BlockSpec(memory_space=pltpu.VMEM), pl.BlockSpec(memory_space=pl.ANY),
+        in_specs=[ANY] * 4 + [SMEM, ANY],
+        out_specs=(pl.BlockSpec(memory_space=pltpu.VMEM), pl.BlockSpec(memory_space=pltpu.VMEM),
                    pl.BlockSpec(memory_space=pltpu.VMEM)) + (pl.BlockSpec(memory_space=pl.ANY),) * len(late),
         scratch_shapes=[
-            pltpu.SemaphoreType.DMA((96,)),
-            pltpu.SemaphoreType.DMA((96,)),
+            pltpu.VMEM((group_size, 3, 1, per_device), jnp.int32),
+            pltpu.VMEM((group_size, 1, per_device), jnp.int32),
+            pltpu.VMEM((1, per_device), jnp.int32),
+            pltpu.SemaphoreType.DMA((104,)),
+            pltpu.SemaphoreType.DMA((104,)),
             pltpu.SemaphoreType.DMA((16,)),
         ],
         compiler_params=pltpu.CompilerParams(
-            collective_id=0, has_side_effects=True, vmem_limit_bytes=2**20),
+            collective_id=0, has_side_effects=True, vmem_limit_bytes=4 * 2**20),
         name="exchange",
-    )(pltpu.with_memory_space_constraint(hop, pltpu.HBM), meta,
-      pltpu.with_memory_space_constraint(vec, pltpu.HBM))
+    )(in_hbm(hop), *map(in_hbm, ints[:3]), ints[3], in_hbm(vec))
 
 
 def bits_of(count):
     return max(1, (count - 1).bit_length())
-
-
-def arrange(meta, bucket, counts, group_size, per_device):
-    stride = group_size * per_device + GROUP
-    for row in range(counts.shape[0]):
-        counts[row] = 0
-
-    def take(i, _):
-        for owner in range(group_size):
-            row = meta[owner, 0, i]
-            held = counts[row]
-            bucket[row * stride + held] = meta[owner, 1, i]
-            counts[row] = held + 1
-        return 0
-
-    lax.fori_loop(0, per_device, take, 0, unroll=8 if per_device % 8 == 0 else 1)
 
 
 def matrix_of(weights, tile, lattice, k):
@@ -268,29 +341,25 @@
         pltpu.matmul_push_rhs(jnp.concatenate(parts, axis=0), staging_register=register, mxu_index=k % 2)
 
 
-def group(bits, size, at, following, bucket, weights, tiles, windows, accs):
-    codes = [bucket[at + j] for j in range(size)]
-    for j, code in enumerate(codes):
-        push(bits, codes[j + 1] if j + 1 < size else bucket[following], windows, len(accs), (j + 1) % 2)
-        index, _, lattice = unpacked(bits, code)
+def group(bits, size, at, plan, weights, tiles, windows, accs):
+    codes = [plan[lax.div(at + j, 128), lax.rem(at + j, 128)] for j in range(size + 1)]
+    for j in range(size):
+        push(bits, codes[j + 1], windows, len(accs), (j + 1) % 2)
+        index, _, lattice = unpacked(bits, codes[j])
         tile = tiles[index].astype(jnp.float32)
         for k, acc in enumerate(accs):
             pltpu.matmul_acc_lhs(acc, matrix_of(weights, tile, lattice, k), load_staged_rhs=j % 2)
 
 
-def every_row(bits, size, row_tiles, first, stride, bucket, counts, weights, tiles, windows, accs, spare, finish, done=None):
+def every_row(bits, size, row_tiles, first, plan, weights, tiles, windows, accs, spare, finish, done=None):
     kpoints = windows[0].shape[0]
     sets = (accs[:kpoints], accs[kpoints:])
+    starts = plan.shape[0] - 1
 
     def one(row, now, before):
-        base = (first + row) * stride
-        groups = jnp.maximum((counts[first + row] + size - 1) // size, 1)
-        after = jnp.minimum(row + 1, row_tiles - 1)
-
-        def follow(g):
-            return jnp.where(g + 1 < groups, base + (g + 1) * size, (first + after) * stride)
-
-        group(bits, size, base, follow(0), bucket, weights, tiles, windows, now)
+        base = plan[starts, first + row]
+        groups = lax.div(plan[starts, first + row + 1] - base, size)
+        group(bits, size, base, plan, weights, tiles, windows, now)
         finish(jnp.maximum(row - 1, 0), [pltpu.matmul_pop(acc) for acc in before])
         if done is not None:
             @pl.when(row > 0)
@@ -298,7 +367,7 @@
                 done(row - 1)
 
         def step(g, _):
-            group(bits, size, base + g * size, follow(g), bucket, weights, tiles, windows, now)
+            group(bits, size, base + g * size, plan, weights, tiles, windows, now)
             return 0
 
         lax.fori_loop(1, groups, step, 0)
@@ -308,7 +377,8 @@
         one(2 * i + 1, sets[1], sets[0])
         return 0
 
-    push(bits, bucket[first * stride], windows, kpoints, 0)
+    at = plan[starts, first]
+    push(bits, plan[lax.div(at, 128), lax.rem(at, 128)], windows, kpoints, 0)
     lax.fori_loop(0, row_tiles // 2, pair, 0)
     if row_tiles % 2:
         one(row_tiles - 1, sets[0], sets[1])
@@ -326,13 +396,8 @@
             + [pltpu.ACC(k % 2)((16, vec_count), jnp.float32) for k in range(kpoints)])
 
 
-def first_kernel(group_size, per_device, row_tiles, bits, pad, meta, weights, tiles, window, total, bucket, counts):
-    kpoints, _, _, edge, vec_count = window.shape
-    stride = group_size * per_device + GROUP
-    arrange(meta, bucket, counts, group_size, per_device)
-    for row in range(2 * row_tiles):
-        for j in range(GROUP):
-            bucket[row * stride + counts[row] + j] = pad
+def first_kernel(bits, plan, weights, tiles, window, total):
+    kpoints, _, row_tiles, edge, vec_count = total.shape
 
     def run(*accs):
         def finish(row, results):
@@ -340,13 +405,12 @@
                 for part in range(2):
                     total[k, part, row] = result[part * edge:(part + 1) * edge]
 
-        every_row(bits, GROUP, row_tiles, 0, stride, bucket, counts, weights, tiles, [window], accs[:-kpoints],
-                  accs[-kpoints:], finish)
+        every_row(bits, GROUP, row_tiles, 0, plan, weights, tiles, [window], accs[:-kpoints], accs[-kpoints:], finish)
 
     pl.run_scoped(run, *accumulators(kpoints, edge, vec_count))
 
 
-def second_kernel(stride, bits, bucket, counts, weights, tiles, total, across, beside, out, stage, out_sem):
+def second_kernel(bits, plan, weights, tiles, total, across, beside, out, stage, out_sem):
     kpoints, _, row_tiles, edge, vec_count = total.shape
 
     def store(row):
@@ -358,7 +422,7 @@
                 for part in range(2):
                     stage[k, part, row] = total[k, part, row] + result[part * edge:(part + 1) * edge]
 
-        every_row(bits, LATE_GROUP, row_tiles, row_tiles, stride, bucket, counts, weights, tiles, [across, beside],
+        every_row(bits, LATE_GROUP, row_tiles, row_tiles, plan, weights, tiles, [across, beside],
                   accs[:-kpoints], accs[-kpoints:], finish, lambda row: store(row).start())
 
     pl.run_scoped(run, *accumulators(kpoints, edge, vec_count))
@@ -366,41 +430,34 @@
         store(row).wait()
 
 
+def in_hbm(x):
+    return pltpu.with_memory_space_constraint(x, pltpu.HBM)
+
+
 def in_vmem(x):
     return pltpu.with_memory_space_constraint(x, pltpu.VMEM)
 
 
-SMEM = pl.BlockSpec(memory_space=pltpu.SMEM)
-VMEM = pl.BlockSpec(memory_space=pltpu.VMEM)
-ANY = pl.BlockSpec(memory_space=pl.ANY)
-
-
-def first_product(per_device, row_tiles, bits, pad, meta, weights, hop, win):
+def first_product(bits, row_tiles, plan, weights, hop, win):
     kpoints, _, _, edge, vec_count = win.shape
-    slots = hop.shape[0]
-    buckets = 2 * row_tiles + 1
-    work = slots * kpoints * 8 * edge * edge * vec_count
+    work = hop.shape[0] * kpoints * 8 * edge * edge * vec_count
     return pl.pallas_call(
-        functools.partial(first_kernel, slots // per_device, per_device, row_tiles, bits, pad),
-        out_shape=(
-            pltpu.VMEM((kpoints, 2, row_tiles, edge, vec_count), jnp.float32),
-            jax.ShapeDtypeStruct((buckets * (slots + GROUP),), jnp.int32),
-            jax.ShapeDtypeStruct((buckets,), jnp.int32),
-        ),
+        functools.partial(first_kernel, bits),
+        out_shape=pltpu.VMEM((kpoints, 2, row_tiles, edge, vec_count), jnp.float32),
         in_specs=[SMEM] * 2 + [VMEM] * 2,
-        out_specs=(VMEM, SMEM, SMEM),
+        out_specs=VMEM,
         compiler_params=pltpu.CompilerParams(vmem_limit_bytes=2**20),
         cost_estimate=pl.CostEstimate(flops=work, bytes_accessed=2**24, transcendentals=0),
         name="first",
-    )(meta, weights, in_vmem(hop), in_vmem(win))
-
-
-def second_product(bits, bucket, counts, weights, hop, total, across, beside):
-    kpoints, _, row_tiles, edge, vec_count = total.shape
+    )(plan, weights, in_vmem(hop), in_vmem(win))
+
+
+def second_product(bits, plan, weights, hop, total, across, beside):
+    row_tiles = total.shape[2]
     return pl.pallas_call(
-        functools.partial(second_kernel, hop.shape[0] + GROUP, bits),
+        functools.partial(second_kernel, bits),
         out_shape=jax.ShapeDtypeStruct(total.shape, jnp.float32),
-        in_specs=[SMEM] * 3 + [VMEM] * 4,
+        in_specs=[SMEM] * 2 + [VMEM] * 4,
         out_specs=ANY,
         scratch_shapes=[
             pltpu.VMEM(total.shape, jnp.float32),
@@ -408,51 +465,30 @@
         ],
         compiler_params=pltpu.CompilerParams(vmem_limit_bytes=12 * 2**20),
         name="second",
-    )(bucket, counts, weights, in_vmem(hop), in_vmem(total), in_vmem(across), in_vmem(beside))
+    )(plan, weights, in_vmem(hop), in_vmem(total), in_vmem(across), in_vmem(beside))
 
 
 def body(hoppings, tile_rows, tile_cols, tile_lats, tile_counts, phase_angle, vectors):
     edge = hoppings.shape[2]
-    per_device = hoppings.shape[1]
     group_size = lax.axis_size("ka")
     row_shards = lax.axis_size("rows")
     kpoints, _, orbitals, vec_count = vectors.shape
     lattices = phase_angle.shape[1]
     row_tiles = orbitals // edge
-    total_tiles = row_tiles * row_shards
-    shard = lax.axis_index("rows")
-    row_start = shard * row_tiles
-    across_tiles, beside_tiles = late_tiles(row_tiles, row_shards)
-    bits = (bits_of(group_size * per_device), bits_of(row_tiles + 2 * BAND))
-
-    lanes = -(-per_device // 128) * 128
-    slot = lax.broadcasted_iota(jnp.int32, (1, per_device), 1)
-    place = jnp.mod(tile_cols - row_start + BAND, total_tiles)
-    low, high = BAND - row_tiles, BAND + 2 * row_tiles
-    even = lax.rem(shard, 2) == 0
-    across_at = place - jnp.where(even, low, high - across_tiles)
-    beside_at = place - jnp.where(even, high - beside_tiles, low)
-    from_across = (across_at >= 0) & (across_at < across_tiles)
-    from_beside = (beside_at >= 0) & (beside_at < beside_tiles)
-    rows = tile_rows - row_start + jnp.where(from_across | from_beside, row_tiles, 0)
-    rows = jnp.where(slot < tile_counts, rows, 2 * row_tiles)
-    place = jnp.where(from_across, across_at, jnp.where(from_beside, across_tiles + beside_at, place))
-    code = (((tile_lats << bits[1]) + place) << bits[0]) + lax.axis_index("ka") * per_device + slot
-    meta = jnp.concatenate([rows, code, jnp.zeros((6, per_device), jnp.int32)], axis=0)
-    meta = jnp.pad(meta, ((0, 0), (0, lanes - per_device)))
+    bits = (bits_of(group_size * hoppings.shape[1]), bits_of(row_tiles + 2 * BAND))
     vec = vectors.reshape(kpoints, 2, row_tiles, edge, vec_count)
     weights = jnp.stack([jnp.cos(phase_angle), jnp.sin(phase_angle)], axis=1).reshape(2 * kpoints, lattices)
-    weights = jnp.pad(weights, ((0, 0), (0, 1)))
-    pad = lattices << (bits[0] + bits[1])
-
-    all_hop, all_meta, win, *late = exchange(group_size, row_shards, hoppings[0], meta, vec)
+    weights = jnp.pad(weights, ((0, 0), (1, 0)))
+
+    ints = (tile_rows, tile_cols, tile_lats, tile_counts)
+    all_hop, plan, win, *late = exchange(group_size, row_shards, bits, hoppings[0], ints, vec)
     if late:
         sign = [1 - 2 * (r % 2) for r in range(row_shards)]
         across = lax.ppermute(late[0], "rows", [(r, (r + 2 * sign[r]) % row_shards) for r in range(row_shards)])
         beside = lax.ppermute(late[1], "rows", [(r, r + sign[r]) for r in range(row_shards)])
-    total, bucket, counts = first_product(per_device, row_tiles, bits, pad, all_meta, weights, all_hop, win)
+    total = first_product(bits, row_tiles, plan, weights, all_hop, win)
     if late:
-        total = second_product(bits, bucket, counts, weights, all_hop, total, across, beside)
+        total = second_product(bits, plan, weights, all_hop, total, across, beside)
     return total.reshape(kpoints, 2, orbitals, vec_count)
 
 

time: 115 us -> 113 us (0.983); the launches traced: 116 us -> 112 us
  Pallas kernels: 112 us -> 105 us
  waiting for transfers between devices: 0.01 us -> 3.88 us
    pallas_call x3, Pallas kernels: 112 us -> 105 us  [the longest x1 77.9 us: exchange(): pl.pallas_call(functools.partial(exchange_kernel, group_size, row_shards,...]
    ppermute x1, waiting for transfers between devices: 0.01 us -> 3.88 us  [body(): lax.ppermute(late[0], 'rows', [(r, (r + 2 * sign[r]) % row_shards) for r...]
  transfers between devices with their start and end apart: 2 -> 2, of which waited for: 0 -> 1; matrix products, arithmetic and copies ran while one was open for 0% -> 0% of each run, Pallas kernels for 23% -> 18%
where the time goes in v4:
time: 113 us; the launch traced here: 112 us
  Pallas kernels  105 us (93%)
  waiting for transfers between devices  3.88 us (3%)
  starting transfers between devices  2.8 us (2%)
    pallas_call x1, Pallas kernels, exchange(): pl.pallas_call(functools.partial(exchange_kernel, group_size, row_shards,...  77.9 us
    pallas_call x1, Pallas kernels, first_product(): pl.pallas_call(functools.partial(first_kernel, bits), out_shape=pltpu.VME...  20.5 us
    pallas_call x1, Pallas kernels, second_product(): pl.pallas_call(functools.partial(second_kernel, bits), out_shape=jax.Shap...  6.38 us
    ppermute x1, waiting for transfers between devices, body(): lax.ppermute(late[0], 'rows', [(r, (r + 2 * sign[r]) % row_shards) for r...  3.88 us
    ppermute x1, starting transfers between devices, body(): lax.ppermute(late[1], 'rows', [(r, r + sign[r]) for r in range(row_shards)])  2.74 us
  transfers between devices with their start and end apart: 2, of which 1 were waited for; matrix products, arithmetic and copies ran while one was open for 0% of the time, Pallas kernels for 18%

profile of v4, /device:TPU:0, one launch (start us, length us, event | category | flops | bytes accessed | tf_op | source)
XLA Modules:
  0.0 112.3 jit_solution(643252474356554895)
XLA Ops:
  0.0 0.0 copy-start
  0.7 77.9 %exchange.1 = (bf16[384,128,128]{2,1,0:T(8,128)(2,1)S(1)}, s32[5,128]{1,0:T(8,128)S(1)}, bf16[2,2,44,128,256]{4,3,2,1,0:T(8,128)(2,1)S(1)}, bf16[2,2,4,128,256]{...) custom-call(bf16[96,128,128]{2,1,0:T(8,128)(2,1)} %bitcast.8, s32[1,96]{1,0:T(1,128)} %tile_rows.1, ...), custom_call_target="tpu_custom_call" | custom-call | tf_op jit(solution)/shard_map/exchange/pallas_call | solution.py:290
  78.6 0.1 collective-permute-start
  78.6 2.7 %collective-permute-start.1 = (bf16[2,2,4,128,256]{4,3,2,1,0:T(8,128)(2,1)S(1)}, bf16[2,2,4,128,256]{4,3,2,1,0:T(8,128)(2,1)S(1)}, u32[]{:S(2)}, u32[]{:S(2)}) collective-permute-start(bf16[2,2,4,128,256]{4,3,2,1,0:T(8,128)(2,1)S(1)} %get-tuple-element.14), channel_id=1, source_target_pairs={{0,1},{1,0},{2,3},{3,2},{4,5},{5,4},{6,7},{7,6},{8,9},{9,8},{10,11... | collective-permute-start | bytes 3145736 | tf_op jit(solution)/shard_map/ppermute | solution.py:488
  81.4 0.0 copy-done
  81.4 0.1 pad.4.weights
  81.5 20.5 %first.1.total = f32[2,2,12,128,256]{4,3,2,1,0:T(8,128)S(1)} custom-call(s32[5,128]{1,0:T(8,128)S(1)} %get-tuple-element.10.plan, f32[4,10]{1,0:T(4,128)S(1)} %pad.4.weights, bf16[384,128,128]{2,1,0:T(8,128)(2,1)S(1)} %get-tuple-element.11.tiles, bf16[2,2,44,128,256]{4,3,2,1,0:T(8,128)(2,1)S(1)} %get-tuple-element.12.window), custom_call_target="tpu_custom_call" | custom-call | flops 25769803776 | bytes 16777216 | tf_op jit(solution)/shard_map/first/pallas_call | solution.py:444
  102.1 3.9 %collective-permute-done.across = bf16[2,2,4,128,256]{4,3,2,1,0:T(8,128)(2,1)S(1)} collective-permute-done((bf16[2,2,4,128,256]{4,3,2,1,0:T(8,128)(2,1)S(1)}, bf16[2,2,4,128,256]{4,3,2,1,0:T(8,128)(2,1)S(1)}, u32[]{:S(2)}, u32[]{:S(2)}) %collective-permute-start) | collective-permute-done | bytes 1048608 | tf_op jit(solution)/shard_map/ppermute | solution.py:487
  105.9 0.0 collective-permute-done.1.beside
  106.0 6.4 %second.1 = f32[2,2,12,128,256]{4,3,2,1,0:T(8,128)} custom-call(s32[5,128]{1,0:T(8,128)S(1)} %get-tuple-element.10.plan, f32[4,10]{1,0:T(4,128)S(1)} %pad.4.weights, bf16[384,128,128]{2,1,0:T(8,128)(2,1)S(1)} %get-tuple-element.11.tiles, f32[2,2,12,128,256]{4,3,2,1,0:T(8,128)S(1)} %first.1.total, ...), custom_call_target="tpu_custom_call" | custom-call | tf_op jit(solution)/shard_map/second/pallas_call | solution.py:457
  (3 shorter events, 0.1 us)
Async XLA Ops:
  0.0 81.4 %copy-start = (f32[2,9]{1,0:T(2,128)S(1)}, f32[2,9]{1,0:T(2,128)}, u32[]{:S(2)}) copy-start(f32[2,9]{1,0:T(2,128)} %param.12) | copy-start | bytes 220
  78.6 27.4 %collective-permute-start = (bf16[2,2,4,128,256]{4,3,2,1,0:T(8,128)(2,1)S(1)}, bf16[2,2,4,128,256]{4,3,2,1,0:T(8,128)(2,1)S(1)}, u32[]{:S(2)}, u32[]{:S(2)}) collective-permute-start(bf16[2,2,4,128,256]{4,3,2,1,0:T(8,128)(2,1)S(1)} %get-tuple-element.13), channel_id=1, source_target_pairs={{0,2},{1,7},{2,4},{3,1},{4,6},{5,3},{6,0},{7,5},{8,10},{9,15},{10,... | collective-permute-start | bytes 3145736 | tf_op jit(solution)/shard_map/ppermute | solution.py:487
  78.6 27.3 %collective-permute-start.1 = (bf16[2,2,4,128,256]{4,3,2,1,0:T(8,128)(2,1)S(1)}, bf16[2,2,4,128,256]{4,3,2,1,0:T(8,128)(2,1)S(1)}, u32[]{:S(2)}, u32[]{:S(2)}) collective-permute-start(bf16[2,2,4,128,256]{4,3,2,1,0:T(8,128)(2,1)S(1)} %get-tuple-element.14), channel_id=1, source_target_pairs={{0,1},{1,0},{2,3},{3,2},{4,5},{5,4},{6,7},{7,6},{8,9},{9,8},{10,11... | collective-permute-start | bytes 3145736 | tf_op jit(solution)/shard_map/ppermute | solution.py:488

commit v5 on v4

--- a/solution.py
+++ b/solution.py
@@ -18,12 +18,19 @@
     return [(start, min(size, total - start)) for start in range(0, total, size)]
 
 
-def late_tiles(row_tiles, row_shards):
+def late_stages(row_tiles, row_shards):
     reach = (BAND + row_tiles - 1) // row_tiles
     if row_tiles > BAND or row_shards % 2 or reach < 2:
-        return 0, 0
+        return []
     extra = min(row_tiles, BAND - row_tiles, row_tiles - 2)
-    return min(extra, row_tiles - extra), extra
+    late = min(extra, row_tiles - extra)
+    first = late - late // 2
+    stages = [(row_tiles - extra - late, first, 0, extra - extra // 2)]
+    if late // 2 and extra // 2:
+        stages.append((row_tiles - extra - late // 2, late // 2, extra - extra // 2, extra // 2))
+    else:
+        stages = [(row_tiles - extra - late, late, 0, extra)]
+    return stages
 
 
 def column(row):
@@ -34,68 +41,95 @@
 
 def make_plan(row_shards, row_tiles, bits, ints, lives, plan):
     group_size, _, _, per_device = ints.shape
-    across_tiles, beside_tiles = late_tiles(row_tiles, row_shards)
+    stages = late_stages(row_tiles, row_shards)
+    dead = (len(stages) + 1) * row_tiles
     shard = lax.axis_index("rows")
     row_start = shard * row_tiles
     total_tiles = row_tiles * row_shards
     odd = lax.rem(shard, 2)
     even = 1 - odd
     low, high = BAND - row_tiles, BAND + 2 * row_tiles
-    across_from = even * low + odd * (high - across_tiles)
-    beside_from = even * (high - beside_tiles) + odd * low
+    extra = sum(stage[3] for stage in stages)
+    main = row_tiles - extra
+    ranges = []
+    for number, (across_at, across_tiles, beside_at, beside_tiles) in enumerate(stages):
+        ranges.append((number + 1, 0, across_tiles,
+                       even * (low + main - across_at - across_tiles) + odd * (high - main + across_at)))
+        ranges.append((number + 1, across_tiles, beside_tiles,
+                       even * (high - extra + beside_at) + odd * (low + extra - beside_at - beside_tiles)))
     lane = lax.broadcasted_iota(jnp.int32, (1, per_device), 1)
 
-    rows, codes, row_cols, code_cols = [], [], [], []
+    rows, keys, row_cols, key_cols, code_cols = [], [], [], [], []
     for owner in range(group_size):
         place = ints[owner, 1] - row_start + BAND
         place = jnp.where(place < 0, place + total_tiles, place)
         place = jnp.where(place >= total_tiles, place - total_tiles, place)
         row = ints[owner, 0] - row_start
-        for begin, count, shift in ((across_from, across_tiles, 0), (beside_from, beside_tiles, across_tiles)):
-            if count:
-                late = (place >= begin) & (place < begin + count) & (row < row_tiles)
-                row = jnp.where(late, row + row_tiles, row)
-                place = jnp.where(late, place - begin + shift, place)
-        row = jnp.where(lane < lives[owner], row, 2 * row_tiles)
+        inside = place
+        for number, shift, count, begin in ranges:
+            late = (inside >= begin) & (inside < begin + count)
+            row = jnp.where(late, row + number * row_tiles, row)
+            place = jnp.where(late, inside - begin + shift, place)
+        row = jnp.where(lane < lives[owner], row, dead)
         code = (((ints[owner, 2] + 1) << bits[1]) + place << bits[0]) + owner * per_device + lane
         rows.append(row.astype(jnp.float32))
-        codes.append(code.astype(jnp.float32))
+        keys.append(((row << bits[1]) + place).astype(jnp.float32))
         row_cols.append(column(rows[-1]))
-        code_cols.append(column(codes[-1]))
+        key_cols.append(column(keys[-1]))
+        code_cols.append(column(code.astype(jnp.float32)))
     row_col = jnp.concatenate(row_cols, axis=0)
+    key_col = jnp.concatenate(key_cols, axis=0)
     code_col = jnp.concatenate(code_cols, axis=0)
     slots = group_size * per_device
-    buckets = -(-(2 * row_tiles + 1) // 8) * 8
+    buckets = -(-(dead + 1) // 8) * 8
     bucket = lax.broadcasted_iota(jnp.int32, (buckets, 1), 0).astype(jnp.float32)
+    index = lax.broadcasted_iota(jnp.int32, (slots, 1), 0)
+    orders, leads = [], []
+    for owner, key in enumerate(keys):
+        ahead = (key_col == key) & (index < lane + owner * per_device)
+        order = jnp.sum(jnp.where(ahead, 1.0, 0.0), axis=0, keepdims=True)
+        live = rows[owner] < dead
+        orders.append(order)
+        leads.append(jnp.where(live & (order - 2 * jnp.floor(order * 0.5) == 0), 1.0, 0.0))
+    order_col = jnp.concatenate([column(order) for order in orders], axis=0)
+    lead_col = jnp.concatenate([column(lead) for lead in leads], axis=0)
+
     held = jnp.zeros((buckets, 1), jnp.float32)
-    for row in rows:
-        held += jnp.sum(jnp.where(bucket == row, 1.0, 0.0), axis=1, keepdims=True)
+    for row, lead in zip(rows, leads):
+        held += jnp.sum(jnp.where(bucket == row, lead, 0.0), axis=1, keepdims=True)
     held = jnp.maximum(held, 1.0)
     held = jnp.where(bucket < row_tiles, jnp.floor((held + (GROUP - 1)) * (1 / GROUP)) * GROUP,
                      jnp.floor((held + (LATE_GROUP - 1)) * (1 / LATE_GROUP)) * LATE_GROUP)
-    index = lax.broadcasted_iota(jnp.int32, (slots, 1), 0)
     spots = []
-    for owner, row in enumerate(rows):
+    for owner, (row, lead) in enumerate(zip(rows, leads)):
         ahead = (row_col == row) & (index < lane + owner * per_device)
-        rank = jnp.sum(jnp.where(ahead, 1.0, 0.0), axis=0, keepdims=True)
+        rank = jnp.sum(jnp.where(ahead, lead_col, 0.0), axis=0, keepdims=True)
         base = jnp.sum(jnp.where(bucket < row, held, 0.0), axis=0, keepdims=True)
-        spots.append(column(jnp.where(row < 2 * row_tiles, base + rank, -1.0)))
+        spots.append(column(jnp.where(lead > 0, base + rank, -1.0)))
     spot = jnp.concatenate(spots, axis=0)
+    seconds = []
+    for row, key, order, lead in zip(rows, keys, orders, leads):
+        led = (key_col == key) & (order_col == order - 1)
+        found = jnp.sum(jnp.where(led, spot, 0.0), axis=0, keepdims=True)
+        seconds.append(column(jnp.where((lead == 0) & (row < dead), found, -1.0)))
+    second = jnp.concatenate(seconds, axis=0)
     wide = lax.broadcasted_iota(jnp.int32, (1, 128), 1)
-    for block in range(plan.shape[0] - 1):
-        here = spot == (wide + block * 128).astype(jnp.float32)
-        plan[block:block + 1] = jnp.sum(jnp.where(here, code_col, 0.0), axis=0, keepdims=True).astype(jnp.int32)
+    blocks = (plan.shape[0] - 1) // 2
+    for block in range(blocks):
+        here = (wide + block * 128).astype(jnp.float32)
+        for line, place in ((block, spot), (blocks + block, second)):
+            picked = jnp.sum(jnp.where(place == here, code_col, 0.0), axis=0, keepdims=True)
+            plan[line:line + 1] = picked.astype(jnp.int32)
     starts = jnp.sum(jnp.where(bucket < wide.astype(jnp.float32), held, 0.0), axis=0, keepdims=True)
     plan[plan.shape[0] - 1:] = starts.astype(jnp.int32)
 
 
 def exchange_kernel(group_size, row_shards, bits, hop, tile_rows, tile_cols, tile_lats, tile_counts, vec,
                     all_hop, plan, win, *rest):
-    across_tiles, beside_tiles = late_tiles(vec.shape[2], row_shards)
-    if across_tiles and beside_tiles:
-        across_out, beside_out, ints, lives, own_lives, send_sem, recv_sem, local_sem = rest
-    else:
-        ints, lives, own_lives, send_sem, recv_sem, local_sem = rest
+    stages = late_stages(vec.shape[2], row_shards)
+    across_tiles = sum(stage[1] for stage in stages)
+    beside_tiles = sum(stage[3] for stage in stages)
+    outs, (ints, lives, own_lives, send_sem, recv_sem, local_sem) = rest[:2 * len(stages)], rest[2 * len(stages):]
 
     slots = hop.shape[0]
     row_tiles = vec.shape[2]
@@ -180,12 +214,14 @@
         extra = min(second, row_tiles - 2)
         main = row_tiles - extra
         kept = main - across_tiles
-        parts = spans(kept, 2) + [(kept + start, count) for start, count in spans(across_tiles, 2)]
+        parts = [(start, count, None) for start, count in spans(kept, 2)]
+        for number, (at, tiles, _, _) in enumerate(stages):
+            parts += [(at + start, count, number) for start, count in spans(tiles, 2)]
 
         def part_tile(parity_even, parity_odd, start, count):
             return parity_even * (extra + start) + parity_odd * (main - start - count)
 
-        near_parts.append(vec_send(part_tile(even, odd, *parts[0]), parts[0][1], sign))
+        near_parts.append(vec_send(part_tile(even, odd, *parts[0][:2]), parts[0][1], sign))
         turned = vec_send(odd * (row_tiles - extra), extra, -2 * sign) if extra else None
     hop_parts = []
     hop_spans = spans(slots, max(1, slots // 12))
@@ -194,7 +230,7 @@
             hop_parts.append((ka + 2 * (h + 1), start, count, send(
                 hop.at[pl.ds(start, count)], all_hop.at[pl.ds(ka * slots + start, count)], at_ka(other))))
     if forwarding:
-        for start, count in parts[1:]:
+        for start, count, _ in parts[1:]:
             near_parts.append(vec_send(part_tile(even, odd, start, count), count, sign))
         if extra and not beside_tiles:
             vec_send(odd * (row_tiles - extra), extra, sign)
@@ -221,33 +257,35 @@
         block = all_hop.at[pl.ds(owner * slots + start, count)]
         send(block, block, at_ka(partner))
 
-    if beside_tiles:
+    holds = []
+    if stages:
         local[2].wait()
-        hold = pltpu.make_async_copy(
-            win.at[:, :, pl.ds(BAND + odd * (row_tiles - beside_tiles), beside_tiles)], beside_out, local_sem.at[3])
-        hold.start()
-        local[2] = hold
+        for number, (_, _, at, count) in enumerate(stages):
+            tile = even * (beside_tiles - at - count) + odd * (row_tiles - beside_tiles + at)
+            holds.append(pltpu.make_async_copy(
+                win.at[:, :, pl.ds(BAND + tile, count)], outs[2 * number + 1], local_sem.at[7 + number]))
+            holds[-1].start()
 
     for copy in about:
         arrived(copy)
     for copy in [local[1]] + local[3:]:
         copy.wait()
-    del local[3:], local[1]
+    local = [local[0]] + (holds or [local[2]])
     make_plan(row_shards, row_tiles, bits, ints, lives, plan)
 
     done = 0
     if forwarding:
         for n, copy in enumerate(near_parts):
             arrived(copy)
-            start, count = parts[n]
+            start, count, number = parts[n]
             tile = part_tile(odd, even, start, count)
-            if start < kept:
+            if number is None:
                 vec_pass(sign, tile, count, 2 * sign)
             else:
-                first = part_tile(odd, even, kept, across_tiles)
+                first = part_tile(odd, even, *stages[number][:2])
                 hold = pltpu.make_async_copy(
                     win.at[:, :, pl.ds(sign * row_tiles + tile + BAND, count)],
-                    across_out.at[:, :, pl.ds(tile - first, count)], local_sem.at[7 + n])
+                    outs[2 * number].at[:, :, pl.ds(tile - first, count)], local_sem.at[10 + n])
                 hold.start()
                 local.append(hold)
             if n == 1 and extra:
@@ -282,16 +320,17 @@
     slots = hop.shape[0]
     per_device = ints[0].shape[1]
     row_tiles = vec.shape[2]
-    blocks = (group_size * per_device + row_tiles * (GROUP + LATE_GROUP)) // 128 + 1
+    blocks = (group_size * per_device + row_tiles * (GROUP + 2 * LATE_GROUP)) // 128 + 1
     width = vec.shape[2] + 2 * BAND
+    stages = late_stages(row_tiles, row_shards)
     late = tuple(
         jax.ShapeDtypeStruct(vec.shape[:2] + (count,) + vec.shape[3:], vec.dtype)
-        for count in late_tiles(vec.shape[2], row_shards) if count)
+        for _, across, _, beside in stages for count in (across, beside))
     return pl.pallas_call(
         functools.partial(exchange_kernel, group_size, row_shards, bits),
         out_shape=(
             pltpu.VMEM((group_size * slots,) + hop.shape[1:], hop.dtype),
-            pltpu.VMEM((blocks + 1, 128), jnp.int32),
+            pltpu.VMEM((2 * blocks + 1, 128), jnp.int32),
             pltpu.VMEM(vec.shape[:2] + (width,) + vec.shape[3:], vec.dtype),
         ) + late,
         in_specs=[ANY] * 4 + [SMEM, ANY],
@@ -303,7 +342,7 @@
             pltpu.VMEM((1, per_device), jnp.int32),
             pltpu.SemaphoreType.DMA((104,)),
             pltpu.SemaphoreType.DMA((104,)),
-            pltpu.SemaphoreType.DMA((16,)),
+            pltpu.SemaphoreType.DMA((24,)),
         ],
         compiler_params=pltpu.CompilerParams(
             collective_id=0, has_side_effects=True, vmem_limit_bytes=4 * 2**20),
@@ -315,9 +354,8 @@
     return max(1, (count - 1).bit_length())
 
 
-def matrix_of(weights, tile, lattice, k):
-    cosine = (weights[2 * k, lattice] * tile).astype(jnp.bfloat16)
-    sine = (weights[2 * k + 1, lattice] * tile).astype(jnp.bfloat16)
+def matrix_of(cosine, sine):
+    cosine, sine = cosine.astype(jnp.bfloat16), sine.astype(jnp.bfloat16)
     return jnp.concatenate(
         [jnp.concatenate([cosine, -sine], axis=1), jnp.concatenate([sine, cosine], axis=1)], axis=0)
 
@@ -342,13 +380,19 @@
 
 
 def group(bits, size, at, plan, weights, tiles, windows, accs):
-    codes = [plan[lax.div(at + j, 128), lax.rem(at + j, 128)] for j in range(size + 1)]
+    blocks = (plan.shape[0] - 1) // 2
+    lines = [(lax.div(at + j, 128), lax.rem(at + j, 128)) for j in range(size + 1)]
+    codes = [plan[line, lane] for line, lane in lines]
     for j in range(size):
         push(bits, codes[j + 1], windows, len(accs), (j + 1) % 2)
         index, _, lattice = unpacked(bits, codes[j])
+        other, _, other_lattice = unpacked(bits, plan[blocks + lines[j][0], lines[j][1]])
         tile = tiles[index].astype(jnp.float32)
+        beside = tiles[other].astype(jnp.float32)
         for k, acc in enumerate(accs):
-            pltpu.matmul_acc_lhs(acc, matrix_of(weights, tile, lattice, k), load_staged_rhs=j % 2)
+            cosine, sine = [weights[2 * k + part, lattice] * tile + weights[2 * k + part, other_lattice] * beside
+                            for part in range(2)]
+            pltpu.matmul_acc_lhs(acc, matrix_of(cosine, sine), load_staged_rhs=j % 2)
 
 
 def every_row(bits, size, row_tiles, first, plan, weights, tiles, windows, accs, spare, finish, done=None):
@@ -410,8 +454,9 @@
     pl.run_scoped(run, *accumulators(kpoints, edge, vec_count))
 
 
-def second_kernel(bits, plan, weights, tiles, total, across, beside, out, stage, out_sem):
+def late_kernel(bits, stage_number, last, plan, weights, tiles, total, across, beside, out, *scratch):
     kpoints, _, row_tiles, edge, vec_count = total.shape
+    stage, out_sem = scratch if last else (out, None)
 
     def store(row):
         return pltpu.make_async_copy(stage.at[:, :, row], out.at[:, :, row], out_sem.at[row])
@@ -422,12 +467,13 @@
                 for part in range(2):
                     stage[k, part, row] = total[k, part, row] + result[part * edge:(part + 1) * edge]
 
-        every_row(bits, LATE_GROUP, row_tiles, row_tiles, plan, weights, tiles, [across, beside],
-                  accs[:-kpoints], accs[-kpoints:], finish, lambda row: store(row).start())
+        every_row(bits, LATE_GROUP, row_tiles, stage_number * row_tiles, plan, weights, tiles, [across, beside],
+                  accs[:-kpoints], accs[-kpoints:], finish, (lambda row: store(row).start()) if last else None)
 
     pl.run_scoped(run, *accumulators(kpoints, edge, vec_count))
-    for row in range(row_tiles):
-        store(row).wait()
+    if last:
+        for row in range(row_tiles):
+            store(row).wait()
 
 
 def in_hbm(x):
@@ -452,19 +498,21 @@
     )(plan, weights, in_vmem(hop), in_vmem(win))
 
 
-def second_product(bits, plan, weights, hop, total, across, beside):
+def late_product(bits, number, last, plan, weights, hop, total, across, beside):
     row_tiles = total.shape[2]
+    work = hop.shape[0] * total.size // 2
     return pl.pallas_call(
-        functools.partial(second_kernel, bits),
-        out_shape=jax.ShapeDtypeStruct(total.shape, jnp.float32),
+        functools.partial(late_kernel, bits, number, last),
+        out_shape=(jax.ShapeDtypeStruct if last else pltpu.VMEM)(total.shape, jnp.float32),
         in_specs=[SMEM] * 2 + [VMEM] * 4,
-        out_specs=ANY,
+        out_specs=ANY if last else VMEM,
         scratch_shapes=[
             pltpu.VMEM(total.shape, jnp.float32),
             pltpu.SemaphoreType.DMA((row_tiles,)),
-        ],
-        compiler_params=pltpu.CompilerParams(vmem_limit_bytes=12 * 2**20),
-        name="second",
+        ] if last else [],
+        compiler_params=pltpu.CompilerParams(vmem_limit_bytes=(12 if last else 2) * 2**20),
+        cost_estimate=pl.CostEstimate(flops=work, bytes_accessed=2**22, transcendentals=0),
+        name="late",
     )(plan, weights, in_vmem(hop), in_vmem(total), in_vmem(across), in_vmem(beside))
 
 
@@ -482,13 +530,13 @@
 
     ints = (tile_rows, tile_cols, tile_lats, tile_counts)
     all_hop, plan, win, *late = exchange(group_size, row_shards, bits, hoppings[0], ints, vec)
-    if late:
-        sign = [1 - 2 * (r % 2) for r in range(row_shards)]
-        across = lax.ppermute(late[0], "rows", [(r, (r + 2 * sign[r]) % row_shards) for r in range(row_shards)])
-        beside = lax.ppermute(late[1], "rows", [(r, r + sign[r]) for r in range(row_shards)])
+    sign = [1 - 2 * (r % 2) for r in range(row_shards)]
+    far = [(r, (r + 2 * sign[r]) % row_shards) for r in range(row_shards)]
+    pairs = [(r, r + sign[r]) for r in range(row_shards)]
+    moved = [lax.ppermute(x, "rows", pairs if n % 2 else far) for n, x in enumerate(late)]
     total = first_product(bits, row_tiles, plan, weights, all_hop, win)
-    if late:
-        total = second_product(bits, plan, weights, all_hop, total, across, beside)
+    for n in range(0, len(moved), 2):
+        total = late_product(bits, n // 2 + 1, n + 2 == len(moved), plan, weights, all_hop, total, *moved[n:n + 2])
     return total.reshape(kpoints, 2, orbitals, vec_count)
 
 

time: 113 us -> 112 us (level)
  starting transfers between devices: 2.8 us -> 5.89 us
  waiting for transfers between devices: 3.88 us -> 1.64 us
  Pallas kernels: 105 us -> 103 us
    pallas_call x1, Pallas kernels: 20.5 us -> 15.6 us  [first_product(): pl.pallas_call(functools.partial(first_kernel, bits), out_shape=pltpu.VME...]
    ppermute x2 -> x4, starting transfers between devices: 2.8 us -> 5.89 us  [body(): lax.ppermute(x, 'rows', pairs if n % 2 else far)]
    pallas_call x1 -> x2, Pallas kernels: 6.38 us -> 8.98 us  [late_product(): pl.pallas_call(functools.partial(late_kernel, bits, number, last), out_sh...]
    ppermute x2 -> x4, waiting for transfers between devices: 3.88 us -> 1.64 us  [body(): lax.ppermute(x, 'rows', pairs if n % 2 else far)]
  transfers between devices with their start and end apart: 2 -> 4, of which waited for: 1 -> 1; matrix products, arithmetic and copies ran while one was open for 0% -> 0% of each run, Pallas kernels for 18% -> 18%
where the time goes in v5:
time: 112 us; the launch traced here: 111 us
  Pallas kernels  103 us (92%)
  starting transfers between devices  5.89 us (5%)
  waiting for transfers between devices  1.64 us (1%)
    pallas_call x1, Pallas kernels, exchange(): pl.pallas_call(functools.partial(exchange_kernel, group_size, row_shards,...  78 us
    pallas_call x1, Pallas kernels, first_product(): pl.pallas_call(functools.partial(first_kernel, bits), out_shape=pltpu.VME...  15.6 us
    pallas_call x2, Pallas kernels, late_product(): pl.pallas_call(functools.partial(late_kernel, bits, number, last), out_sh...  8.98 us
    ppermute x4, starting transfers between devices, body(): lax.ppermute(x, 'rows', pairs if n % 2 else far)  5.89 us
  transfers between devices with their start and end apart: 4, of which 1 were waited for; matrix products, arithmetic and copies ran while one was open for 0% of the time, Pallas kernels for 18%

profile of v5, /device:TPU:0, one launch (start us, length us, event | category | flops | bytes accessed | tf_op | source)
XLA Modules:
  0.0 110.9 jit_solution(12360671638606430904)
XLA Ops:
  0.0 0.0 copy-start
  0.7 78.0 %exchange.1 = (bf16[384,128,128]{2,1,0:T(8,128)(2,1)S(1)}, s32[9,128]{1,0:T(8,128)S(1)}, bf16[2,2,44,128,256]{4,3,2,1,0:T(8,128)(2,1)S(1)}, bf16[2,2,2,128,256]{...) custom-call(bf16[96,128,128]{2,1,0:T(8,128)(2,1)} %bitcast.8, ...), custom_call_target="tpu_custom_call" | custom-call | tf_op jit(solution)/shard_map/exchange/pallas_call | solution.py:329
  78.6 0.1 collective-permute-start
  78.7 2.7 %collective-permute-start.1 = (bf16[2,2,2,128,256]{4,3,2,1,0:T(8,128)(2,1)S(1)}, bf16[2,2,2,128,256]{4,3,2,1,0:T(8,128)(2,1)S(1)}, u32[]{:S(2)}, u32[]{:S(2)}) collective-permute-start(bf16[2,2,2,128,256]{4,3,2,1,0:T(8,128)(2,1)S(1)} %get-tuple-element.16), channel_id=1, source_target_pairs={{0,1},{1,0},{2,3},{3,2},{4,5},{5,4},{6,7},{7,6},{8,9},{9,8},{10,11... | collective-permute-start | bytes 1572872 | tf_op jit(solution)/shard_map/ppermute | solution.py:536
  81.4 0.8 collective-permute-start.2
  82.2 2.3 %collective-permute-start.3 = (bf16[2,2,2,128,256]{4,3,2,1,0:T(8,128)(2,1)S(1)}, bf16[2,2,2,128,256]{4,3,2,1,0:T(8,128)(2,1)S(1)}, u32[]{:S(2)}, u32[]{:S(2)}) collective-permute-start(bf16[2,2,2,128,256]{4,3,2,1,0:T(8,128)(2,1)S(1)} %get-tuple-element.18), channel_id=1, source_target_pairs={{0,1},{1,0},{2,3},{3,2},{4,5},{5,4},{6,7},{7,6},{8,9},{9,8},{10,11... | collective-permute-start | bytes 1572872 | tf_op jit(solution)/shard_map/ppermute | solution.py:536
  84.5 0.0 copy-done
  84.6 0.1 pad.4.weights
  84.7 15.6 %first.1.total = f32[2,2,12,128,256]{4,3,2,1,0:T(8,128)S(1)} custom-call(s32[9,128]{1,0:T(8,128)S(1)} %get-tuple-element.12.plan, f32[4,10]{1,0:T(4,128)S(1)} %pad.4.weights, bf16[384,128,128]{2,1,0:T(8,128)(2,1)S(1)} %get-tuple-element.13.tiles, bf16[2,2,44,128,256]{4,3,2,1,0:T(8,128)(2,1)S(1)} %get-tuple-element.14.window), custom_call_target="tpu_custom_call" | custom-call | flops 25769803776 | bytes 16777216 | tf_op jit(solution)/shard_map/first/pallas_call | solution.py:490
  100.3 0.0 collective-permute-done.across
  100.3 0.0 collective-permute-done.1.beside
  100.3 4.1 %late.2.total = f32[2,2,12,128,256]{4,3,2,1,0:T(8,128)S(1)} custom-call(s32[9,128]{1,0:T(8,128)S(1)} %get-tuple-element.12.plan, f32[4,10]{1,0:T(4,128)S(1)} %pad.4.weights, bf16[384,128,128]{2,1,0:T(8,128)(2,1)S(1)} %get-tuple-element.13.tiles, f32[2,2,12,128,256]{4,3,2,1,0:T(8,128)S(1)} %first.1.total, ...), custom_call_target="tpu_custom_call" | custom-call | flops 301989888 | bytes 4194304 | tf_op jit(solution)/shard_map/late/pallas_call | solution.py:504
  104.4 1.6 %collective-permute-done.2.across = bf16[2,2,2,128,256]{4,3,2,1,0:T(8,128)(2,1)S(1)} collective-permute-done((bf16[2,2,2,128,256]{4,3,2,1,0:T(8,128)(2,1)S(1)}, bf16[2,2,2,128,256]{4,3,2,1,0:T(8,128)(2,1)S(1)}, u32[]{:S(2)}, u32[]{:S(2)}) %collective-permute-start.2) | collective-permute-done | bytes 524320 | tf_op jit(solution)/shard_map/ppermute | solution.py:536
  106.0 0.0 collective-permute-done.3.beside
  106.0 4.9 %late.3 = f32[2,2,12,128,256]{4,3,2,1,0:T(8,128)} custom-call(s32[9,128]{1,0:T(8,128)S(1)} %get-tuple-element.12.plan, f32[4,10]{1,0:T(4,128)S(1)} %pad.4.weights, bf16[384,128,128]{2,1,0:T(8,128)(2,1)S(1)} %get-tuple-element.13.tiles, f32[2,2,12,128,256]{4,3,2,1,0:T(8,128)S(1)} %late.2.total, ...), custom_call_target="tpu_custom_call" | custom-call | flops 301989888 | bytes 4194304 | tf_op jit(solution)/shard_map/late/pallas_call | solution.py:504
  (3 shorter events, 0.1 us)
Async XLA Ops:
  0.0 84.5 %copy-start = (f32[2,9]{1,0:T(2,128)S(1)}, f32[2,9]{1,0:T(2,128)}, u32[]{:S(2)}) copy-start(f32[2,9]{1,0:T(2,128)} %param.12) | copy-start | bytes 220
  78.6 21.6 %collective-permute-start = (bf16[2,2,2,128,256]{4,3,2,1,0:T(8,128)(2,1)S(1)}, bf16[2,2,2,128,256]{4,3,2,1,0:T(8,128)(2,1)S(1)}, u32[]{:S(2)}, u32[]{:S(2)}) collective-permute-start(bf16[2,2,2,128,256]{4,3,2,1,0:T(8,128)(2,1)S(1)} %get-tuple-element.15), channel_id=1, source_target_pairs={{0,2},{1,7},{2,4},{3,1},{4,6},{5,3},{6,0},{7,5},{8,10},{9,15},{10,... | collective-permute-start | bytes 1572872 | tf_op jit(solution)/shard_map/ppermute | solution.py:536
  78.7 21.6 %collective-permute-start.1 = (bf16[2,2,2,128,256]{4,3,2,1,0:T(8,128)(2,1)S(1)}, bf16[2,2,2,128,256]{4,3,2,1,0:T(8,128)(2,1)S(1)}, u32[]{:S(2)}, u32[]{:S(2)}) collective-permute-start(bf16[2,2,2,128,256]{4,3,2,1,0:T(8,128)(2,1)S(1)} %get-tuple-element.16), channel_id=1, source_target_pairs={{0,1},{1,0},{2,3},{3,2},{4,5},{5,4},{6,7},{7,6},{8,9},{9,8},{10,11... | collective-permute-start | bytes 1572872 | tf_op jit(solution)/shard_map/ppermute | solution.py:536
  81.4 24.6 %collective-permute-start.2 = (bf16[2,2,2,128,256]{4,3,2,1,0:T(8,128)(2,1)S(1)}, bf16[2,2,2,128,256]{4,3,2,1,0:T(8,128)(2,1)S(1)}, u32[]{:S(2)}, u32[]{:S(2)}) collective-permute-start(bf16[2,2,2,128,256]{4,3,2,1,0:T(8,128)(2,1)S(1)} %get-tuple-element.17), channel_id=1, source_target_pairs={{0,2},{1,7},{2,4},{3,1},{4,6},{5,3},{6,0},{7,5},{8,10},{9,15},{10,... | collective-permute-start | bytes 1572872 | tf_op jit(solution)/shard_map/ppermute | solution.py:536
  82.2 23.8 %collective-permute-start.3 = (bf16[2,2,2,128,256]{4,3,2,1,0:T(8,128)(2,1)S(1)}, bf16[2,2,2,128,256]{4,3,2,1,0:T(8,128)(2,1)S(1)}, u32[]{:S(2)}, u32[]{:S(2)}) collective-permute-start(bf16[2,2,2,128,256]{4,3,2,1,0:T(8,128)(2,1)S(1)} %get-tuple-element.18), channel_id=1, source_target_pairs={{0,1},{1,0},{2,3},{3,2},{4,5},{5,4},{6,7},{7,6},{8,9},{9,8},{10,11... | collective-permute-start | bytes 1572872 | tf_op jit(solution)/shard_map/ppermute | solution.py:536

commit v6 on v5

--- a/solution.py
+++ b/solution.py
@@ -10,7 +10,7 @@
 NLAT = 9
 BAND = 16
 GROUP = 4
-LATE_GROUP = 2
+LATE_GROUP = 1
 MESH = pl.DeviceIdType.MESH
 
 
@@ -224,7 +224,7 @@
         near_parts.append(vec_send(part_tile(even, odd, *parts[0][:2]), parts[0][1], sign))
         turned = vec_send(odd * (row_tiles - extra), extra, -2 * sign) if extra else None
     hop_parts = []
-    hop_spans = spans(slots, max(1, slots // 12))
+    hop_spans = spans(slots, max(1, slots // 24))
     for h, other in enumerate(across):
         for start, count in hop_spans:
             hop_parts.append((ka + 2 * (h + 1), start, count, send(
@@ -384,7 +384,8 @@
     lines = [(lax.div(at + j, 128), lax.rem(at + j, 128)) for j in range(size + 1)]
     codes = [plan[line, lane] for line, lane in lines]
     for j in range(size):
-        push(bits, codes[j + 1], windows, len(accs), (j + 1) % 2)
+        if size > 1:
+            push(bits, codes[j + 1], windows, len(accs), (j + 1) % 2)
         index, _, lattice = unpacked(bits, codes[j])
         other, _, other_lattice = unpacked(bits, plan[blocks + lines[j][0], lines[j][1]])
         tile = tiles[index].astype(jnp.float32)
@@ -393,6 +394,8 @@
             cosine, sine = [weights[2 * k + part, lattice] * tile + weights[2 * k + part, other_lattice] * beside
                             for part in range(2)]
             pltpu.matmul_acc_lhs(acc, matrix_of(cosine, sine), load_staged_rhs=j % 2)
+    if size == 1:
+        push(bits, codes[1], windows, len(accs), 0)
 
 
 def every_row(bits, size, row_tiles, first, plan, weights, tiles, windows, accs, spare, finish, done=None):

time: 112 us -> 110 us (0.982)
    pallas_call x2, Pallas kernels: 8.98 us -> 7.29 us  [late_product(): pl.pallas_call(functools.partial(late_kernel, bits, number, last), out_sh...]
where the time goes in v6:
time: 110 us
  Pallas kernels  102 us (93%)
  starting transfers between devices  5.89 us (5%)
  waiting for transfers between devices  1.65 us (2%)
    pallas_call x1, Pallas kernels, exchange(): pl.pallas_call(functools.partial(exchange_kernel, group_size, row_shards,...  77.8 us
    pallas_call x1, Pallas kernels, first_product(): pl.pallas_call(functools.partial(first_kernel, bits), out_shape=pltpu.VME...  16.5 us
    pallas_call x2, Pallas kernels, late_product(): pl.pallas_call(functools.partial(late_kernel, bits, number, last), out_sh...  7.29 us
    ppermute x4, starting transfers between devices, body(): lax.ppermute(x, 'rows', pairs if n % 2 else far)  5.89 us
  transfers between devices with their start and end apart: 4, of which 1 were waited for; matrix products, arithmetic and copies ran while one was open for 0% of the time, Pallas kernels for 18%

profile of v6, /device:TPU:0, one launch (start us, length us, event | category | flops | bytes accessed | tf_op | source)
XLA Modules:
  0.0 110.0 jit_solution(17492434062166697183)
XLA Ops:
  0.0 0.0 copy-start
  0.7 77.8 %exchange.1 = (bf16[384,128,128]{2,1,0:T(8,128)(2,1)S(1)}, s32[9,128]{1,0:T(8,128)S(1)}, bf16[2,2,44,128,256]{4,3,2,1,0:T(8,128)(2,1)S(1)}, bf16[2,2,2,128,256]{...) custom-call(bf16[96,128,128]{2,1,0:T(8,128)(2,1)} %bitcast.8, ...), custom_call_target="tpu_custom_call" | custom-call | tf_op jit(solution)/shard_map/exchange/pallas_call | solution.py:329
  78.5 0.1 collective-permute-start
  78.5 3.0 %collective-permute-start.1 = (bf16[2,2,2,128,256]{4,3,2,1,0:T(8,128)(2,1)S(1)}, bf16[2,2,2,128,256]{4,3,2,1,0:T(8,128)(2,1)S(1)}, u32[]{:S(2)}, u32[]{:S(2)}) collective-permute-start(bf16[2,2,2,128,256]{4,3,2,1,0:T(8,128)(2,1)S(1)} %get-tuple-element.16), channel_id=1, source_target_pairs={{0,1},{1,0},{2,3},{3,2},{4,5},{5,4},{6,7},{7,6},{8,9},{9,8},{10,11... | collective-permute-start | bytes 1572872 | tf_op jit(solution)/shard_map/ppermute | solution.py:539
  81.5 0.5 collective-permute-start.2
  82.1 2.3 %collective-permute-start.3 = (bf16[2,2,2,128,256]{4,3,2,1,0:T(8,128)(2,1)S(1)}, bf16[2,2,2,128,256]{4,3,2,1,0:T(8,128)(2,1)S(1)}, u32[]{:S(2)}, u32[]{:S(2)}) collective-permute-start(bf16[2,2,2,128,256]{4,3,2,1,0:T(8,128)(2,1)S(1)} %get-tuple-element.18), channel_id=1, source_target_pairs={{0,1},{1,0},{2,3},{3,2},{4,5},{5,4},{6,7},{7,6},{8,9},{9,8},{10,11... | collective-permute-start | bytes 1572872 | tf_op jit(solution)/shard_map/ppermute | solution.py:539
  84.4 0.0 copy-done
  84.4 0.1 pad.4.weights
  84.5 16.5 %first.1.total = f32[2,2,12,128,256]{4,3,2,1,0:T(8,128)S(1)} custom-call(s32[9,128]{1,0:T(8,128)S(1)} %get-tuple-element.12.plan, f32[4,10]{1,0:T(4,128)S(1)} %pad.4.weights, bf16[384,128,128]{2,1,0:T(8,128)(2,1)S(1)} %get-tuple-element.13.tiles, bf16[2,2,44,128,256]{4,3,2,1,0:T(8,128)(2,1)S(1)} %get-tuple-element.14.window), custom_call_target="tpu_custom_call" | custom-call | flops 25769803776 | bytes 16777216 | tf_op jit(solution)/shard_map/first/pallas_call | solution.py:493
  101.1 0.0 collective-permute-done.across
  101.1 0.0 collective-permute-done.1.beside
  101.1 3.2 %late.2.total = f32[2,2,12,128,256]{4,3,2,1,0:T(8,128)S(1)} custom-call(s32[9,128]{1,0:T(8,128)S(1)} %get-tuple-element.12.plan, f32[4,10]{1,0:T(4,128)S(1)} %pad.4.weights, bf16[384,128,128]{2,1,0:T(8,128)(2,1)S(1)} %get-tuple-element.13.tiles, f32[2,2,12,128,256]{4,3,2,1,0:T(8,128)S(1)} %first.1.total, ...), custom_call_target="tpu_custom_call" | custom-call | flops 301989888 | bytes 4194304 | tf_op jit(solution)/shard_map/late/pallas_call | solution.py:507
  104.2 1.6 %collective-permute-done.2.across = bf16[2,2,2,128,256]{4,3,2,1,0:T(8,128)(2,1)S(1)} collective-permute-done((bf16[2,2,2,128,256]{4,3,2,1,0:T(8,128)(2,1)S(1)}, bf16[2,2,2,128,256]{4,3,2,1,0:T(8,128)(2,1)S(1)}, u32[]{:S(2)}, u32[]{:S(2)}) %collective-permute-start.2) | collective-permute-done | bytes 524320 | tf_op jit(solution)/shard_map/ppermute | solution.py:539
  105.9 0.0 collective-permute-done.3.beside
  105.9 4.1 %late.3 = f32[2,2,12,128,256]{4,3,2,1,0:T(8,128)} custom-call(s32[9,128]{1,0:T(8,128)S(1)} %get-tuple-element.12.plan, f32[4,10]{1,0:T(4,128)S(1)} %pad.4.weights, bf16[384,128,128]{2,1,0:T(8,128)(2,1)S(1)} %get-tuple-element.13.tiles, f32[2,2,12,128,256]{4,3,2,1,0:T(8,128)S(1)} %late.2.total, ...), custom_call_target="tpu_custom_call" | custom-call | flops 301989888 | bytes 4194304 | tf_op jit(solution)/shard_map/late/pallas_call | solution.py:507
  (3 shorter events, 0.1 us)
Async XLA Ops:
  0.0 84.4 %copy-start = (f32[2,9]{1,0:T(2,128)S(1)}, f32[2,9]{1,0:T(2,128)}, u32[]{:S(2)}) copy-start(f32[2,9]{1,0:T(2,128)} %param.12) | copy-start | bytes 220
  78.5 22.6 %collective-permute-start = (bf16[2,2,2,128,256]{4,3,2,1,0:T(8,128)(2,1)S(1)}, bf16[2,2,2,128,256]{4,3,2,1,0:T(8,128)(2,1)S(1)}, u32[]{:S(2)}, u32[]{:S(2)}) collective-permute-start(bf16[2,2,2,128,256]{4,3,2,1,0:T(8,128)(2,1)S(1)} %get-tuple-element.15), channel_id=1, source_target_pairs={{0,2},{1,7},{2,4},{3,1},{4,6},{5,3},{6,0},{7,5},{8,10},{9,15},{10,... | collective-permute-start | bytes 1572872 | tf_op jit(solution)/shard_map/ppermute | solution.py:539
  78.5 22.5 %collective-permute-start.1 = (bf16[2,2,2,128,256]{4,3,2,1,0:T(8,128)(2,1)S(1)}, bf16[2,2,2,128,256]{4,3,2,1,0:T(8,128)(2,1)S(1)}, u32[]{:S(2)}, u32[]{:S(2)}) collective-permute-start(bf16[2,2,2,128,256]{4,3,2,1,0:T(8,128)(2,1)S(1)} %get-tuple-element.16), channel_id=1, source_target_pairs={{0,1},{1,0},{2,3},{3,2},{4,5},{5,4},{6,7},{7,6},{8,9},{9,8},{10,11... | collective-permute-start | bytes 1572872 | tf_op jit(solution)/shard_map/ppermute | solution.py:539
  81.5 24.4 %collective-permute-start.2 = (bf16[2,2,2,128,256]{4,3,2,1,0:T(8,128)(2,1)S(1)}, bf16[2,2,2,128,256]{4,3,2,1,0:T(8,128)(2,1)S(1)}, u32[]{:S(2)}, u32[]{:S(2)}) collective-permute-start(bf16[2,2,2,128,256]{4,3,2,1,0:T(8,128)(2,1)S(1)} %get-tuple-element.17), channel_id=1, source_target_pairs={{0,2},{1,7},{2,4},{3,1},{4,6},{5,3},{6,0},{7,5},{8,10},{9,15},{10,... | collective-permute-start | bytes 1572872 | tf_op jit(solution)/shard_map/ppermute | solution.py:539
  82.1 23.8 %collective-permute-start.3 = (bf16[2,2,2,128,256]{4,3,2,1,0:T(8,128)(2,1)S(1)}, bf16[2,2,2,128,256]{4,3,2,1,0:T(8,128)(2,1)S(1)}, u32[]{:S(2)}, u32[]{:S(2)}) collective-permute-start(bf16[2,2,2,128,256]{4,3,2,1,0:T(8,128)(2,1)S(1)} %get-tuple-element.18), channel_id=1, source_target_pairs={{0,1},{1,0},{2,3},{3,2},{4,5},{5,4},{6,7},{7,6},{8,9},{9,8},{10,11... | collective-permute-start | bytes 1572872 | tf_op jit(solution)/shard_map/ppermute | solution.py:539

commit v7 on v6

--- a/solution.py
+++ b/solution.py
@@ -224,7 +224,13 @@
         near_parts.append(vec_send(part_tile(even, odd, *parts[0][:2]), parts[0][1], sign))
         turned = vec_send(odd * (row_tiles - extra), extra, -2 * sign) if extra else None
     hop_parts = []
-    hop_spans = spans(slots, max(1, slots // 24))
+    size = max(1, slots // 8)
+    hop_spans = spans(slots - size, size)
+    start = slots - size
+    while start < slots:
+        size = min((size + 1) // 2, slots - start)
+        hop_spans.append((start, size))
+        start += size
     for h, other in enumerate(across):
         for start, count in hop_spans:
             hop_parts.append((ka + 2 * (h + 1), start, count, send(

time: 110 us -> 110 us (level)
  transfers between devices with their start and end apart: 4 -> 4, of which waited for: 1 -> 1; matrix products, arithmetic and copies ran while one was open for 0% -> 0% of each run, Pallas kernels for 18% -> 17%
where the time goes in v7:
time: 110 us
  Pallas kernels  101 us (92%)
  starting transfers between devices  5.89 us (5%)
  waiting for transfers between devices  2.52 us (2%)
    pallas_call x1, Pallas kernels, exchange(): pl.pallas_call(functools.partial(exchange_kernel, group_size, row_shards,...  77.7 us
    pallas_call x1, Pallas kernels, first_product(): pl.pallas_call(functools.partial(first_kernel, bits), out_shape=pltpu.VME...  15.6 us
    pallas_call x2, Pallas kernels, late_product(): pl.pallas_call(functools.partial(late_kernel, bits, number, last), out_sh...  7.6 us
    ppermute x4, starting transfers between devices, body(): lax.ppermute(x, 'rows', pairs if n % 2 else far)  5.89 us
    ppermute x4, waiting for transfers between devices, body(): lax.ppermute(x, 'rows', pairs if n % 2 else far)  2.52 us
  transfers between devices with their start and end apart: 4, of which 1 were waited for; matrix products, arithmetic and copies ran while one was open for 0% of the time, Pallas kernels for 17%

profile of v7, /device:TPU:0, one launch (start us, length us, event | category | flops | bytes accessed | tf_op | source)
XLA Modules:
  0.0 110.1 jit_solution(18299472762702851206)
XLA Ops:
  0.0 0.0 copy-start
  0.7 77.7 %exchange.1 = (bf16[384,128,128]{2,1,0:T(8,128)(2,1)S(1)}, s32[9,128]{1,0:T(8,128)S(1)}, bf16[2,2,44,128,256]{4,3,2,1,0:T(8,128)(2,1)S(1)}, bf16[2,2,2,128,256]{...) custom-call(bf16[96,128,128]{2,1,0:T(8,128)(2,1)} %bitcast.8, ...), custom_call_target="tpu_custom_call" | custom-call | tf_op jit(solution)/shard_map/exchange/pallas_call | solution.py:335
  78.3 0.1 collective-permute-start
  78.4 3.0 %collective-permute-start.1 = (bf16[2,2,2,128,256]{4,3,2,1,0:T(8,128)(2,1)S(1)}, bf16[2,2,2,128,256]{4,3,2,1,0:T(8,128)(2,1)S(1)}, u32[]{:S(2)}, u32[]{:S(2)}) collective-permute-start(bf16[2,2,2,128,256]{4,3,2,1,0:T(8,128)(2,1)S(1)} %get-tuple-element.16), channel_id=1, source_target_pairs={{0,1},{1,0},{2,3},{3,2},{4,5},{5,4},{6,7},{7,6},{8,9},{9,8},{10,11... | collective-permute-start | bytes 1572872 | tf_op jit(solution)/shard_map/ppermute | solution.py:545
  81.4 0.5 collective-permute-start.2
  81.9 2.3 %collective-permute-start.3 = (bf16[2,2,2,128,256]{4,3,2,1,0:T(8,128)(2,1)S(1)}, bf16[2,2,2,128,256]{4,3,2,1,0:T(8,128)(2,1)S(1)}, u32[]{:S(2)}, u32[]{:S(2)}) collective-permute-start(bf16[2,2,2,128,256]{4,3,2,1,0:T(8,128)(2,1)S(1)} %get-tuple-element.18), channel_id=1, source_target_pairs={{0,1},{1,0},{2,3},{3,2},{4,5},{5,4},{6,7},{7,6},{8,9},{9,8},{10,11... | collective-permute-start | bytes 1572872 | tf_op jit(solution)/shard_map/ppermute | solution.py:545
  84.2 0.0 copy-done
  84.3 0.1 pad.4.weights
  84.4 15.6 %first.1.total = f32[2,2,12,128,256]{4,3,2,1,0:T(8,128)S(1)} custom-call(s32[9,128]{1,0:T(8,128)S(1)} %get-tuple-element.12.plan, f32[4,10]{1,0:T(4,128)S(1)} %pad.4.weights, bf16[384,128,128]{2,1,0:T(8,128)(2,1)S(1)} %get-tuple-element.13.tiles, bf16[2,2,44,128,256]{4,3,2,1,0:T(8,128)(2,1)S(1)} %get-tuple-element.14.window), custom_call_target="tpu_custom_call" | custom-call | flops 25769803776 | bytes 16777216 | tf_op jit(solution)/shard_map/first/pallas_call | solution.py:499
  100.0 0.0 collective-permute-done.across
  100.0 0.0 collective-permute-done.1.beside
  100.0 3.2 %late.2.total = f32[2,2,12,128,256]{4,3,2,1,0:T(8,128)S(1)} custom-call(s32[9,128]{1,0:T(8,128)S(1)} %get-tuple-element.12.plan, f32[4,10]{1,0:T(4,128)S(1)} %pad.4.weights, bf16[384,128,128]{2,1,0:T(8,128)(2,1)S(1)} %get-tuple-element.13.tiles, f32[2,2,12,128,256]{4,3,2,1,0:T(8,128)S(1)} %first.1.total, ...), custom_call_target="tpu_custom_call" | custom-call | flops 301989888 | bytes 4194304 | tf_op jit(solution)/shard_map/late/pallas_call | solution.py:513
  103.2 2.5 %collective-permute-done.2.across = bf16[2,2,2,128,256]{4,3,2,1,0:T(8,128)(2,1)S(1)} collective-permute-done((bf16[2,2,2,128,256]{4,3,2,1,0:T(8,128)(2,1)S(1)}, bf16[2,2,2,128,256]{4,3,2,1,0:T(8,128)(2,1)S(1)}, u32[]{:S(2)}, u32[]{:S(2)}) %collective-permute-start.2) | collective-permute-done | bytes 524320 | tf_op jit(solution)/shard_map/ppermute | solution.py:545
  105.7 0.0 collective-permute-done.3.beside
  105.7 4.4 %late.3 = f32[2,2,12,128,256]{4,3,2,1,0:T(8,128)} custom-call(s32[9,128]{1,0:T(8,128)S(1)} %get-tuple-element.12.plan, f32[4,10]{1,0:T(4,128)S(1)} %pad.4.weights, bf16[384,128,128]{2,1,0:T(8,128)(2,1)S(1)} %get-tuple-element.13.tiles, f32[2,2,12,128,256]{4,3,2,1,0:T(8,128)S(1)} %late.2.total, ...), custom_call_target="tpu_custom_call" | custom-call | flops 301989888 | bytes 4194304 | tf_op jit(solution)/shard_map/late/pallas_call | solution.py:513
  (3 shorter events, 0.1 us)
Async XLA Ops:
  0.0 84.2 %copy-start = (f32[2,9]{1,0:T(2,128)S(1)}, f32[2,9]{1,0:T(2,128)}, u32[]{:S(2)}) copy-start(f32[2,9]{1,0:T(2,128)} %param.12) | copy-start | bytes 220
  78.3 21.6 %collective-permute-start = (bf16[2,2,2,128,256]{4,3,2,1,0:T(8,128)(2,1)S(1)}, bf16[2,2,2,128,256]{4,3,2,1,0:T(8,128)(2,1)S(1)}, u32[]{:S(2)}, u32[]{:S(2)}) collective-permute-start(bf16[2,2,2,128,256]{4,3,2,1,0:T(8,128)(2,1)S(1)} %get-tuple-element.15), channel_id=1, source_target_pairs={{0,2},{1,7},{2,4},{3,1},{4,6},{5,3},{6,0},{7,5},{8,10},{9,15},{10,... | collective-permute-start | bytes 1572872 | tf_op jit(solution)/shard_map/ppermute | solution.py:545
  78.4 21.6 %collective-permute-start.1 = (bf16[2,2,2,128,256]{4,3,2,1,0:T(8,128)(2,1)S(1)}, bf16[2,2,2,128,256]{4,3,2,1,0:T(8,128)(2,1)S(1)}, u32[]{:S(2)}, u32[]{:S(2)}) collective-permute-start(bf16[2,2,2,128,256]{4,3,2,1,0:T(8,128)(2,1)S(1)} %get-tuple-element.16), channel_id=1, source_target_pairs={{0,1},{1,0},{2,3},{3,2},{4,5},{5,4},{6,7},{7,6},{8,9},{9,8},{10,11... | collective-permute-start | bytes 1572872 | tf_op jit(solution)/shard_map/ppermute | solution.py:545
  81.4 24.2 %collective-permute-start.2 = (bf16[2,2,2,128,256]{4,3,2,1,0:T(8,128)(2,1)S(1)}, bf16[2,2,2,128,256]{4,3,2,1,0:T(8,128)(2,1)S(1)}, u32[]{:S(2)}, u32[]{:S(2)}) collective-permute-start(bf16[2,2,2,128,256]{4,3,2,1,0:T(8,128)(2,1)S(1)} %get-tuple-element.17), channel_id=1, source_target_pairs={{0,2},{1,7},{2,4},{3,1},{4,6},{5,3},{6,0},{7,5},{8,10},{9,15},{10,... | collective-permute-start | bytes 1572872 | tf_op jit(solution)/shard_map/ppermute | solution.py:545
  81.9 23.8 %collective-permute-start.3 = (bf16[2,2,2,128,256]{4,3,2,1,0:T(8,128)(2,1)S(1)}, bf16[2,2,2,128,256]{4,3,2,1,0:T(8,128)(2,1)S(1)}, u32[]{:S(2)}, u32[]{:S(2)}) collective-permute-start(bf16[2,2,2,128,256]{4,3,2,1,0:T(8,128)(2,1)S(1)} %get-tuple-element.18), channel_id=1, source_target_pairs={{0,1},{1,0},{2,3},{3,2},{4,5},{5,4},{6,7},{7,6},{8,9},{9,8},{10,11... | collective-permute-start | bytes 1572872 | tf_op jit(solution)/shard_map/ppermute | solution.py:545
